TPU v7x, 32 devices: a whole 2x2x4 slice. The times are simulated.
32 devices in a mesh: groups: 2 (over y), seq: 4 (over x, core), tensor: 4 (over z).
Axes of the slice: x: 2, y: 2, z: 4, core: 2. Of those that a mesh axis runs over, the one named last changes fastest.
Arguments:
- hidden: bfloat16 [256, 4608], P(('groups', 'seq')), parts along dimension 0, may hold values from -6 to 6
- pre_gain: float32 [4608], replicated, may hold values from 0.25 to 1.75
- w_query: bfloat16 [4608, 4096], P(None, 'tensor'), may hold values from -0.09375 to 0.09375
- w_key: bfloat16 [4608, 2048], P(None, 'tensor'), may hold values from -0.09375 to 0.09375
- w_value: bfloat16 [4608, 2048], P(None, 'tensor'), may hold values from -0.09375 to 0.09375
- w_out: bfloat16 [4096, 4608], P('tensor'), may hold values from -0.125 to 0.125
- post_gain: float32 [4608], P('tensor'), may hold values from 0.25 to 1.75
- cache_pool: bfloat16 [512, 2, 128, 2048], P(('groups', 'seq'), None, None, 'tensor'), parts along dimension 0, may hold values from -6 to 6
- prompt_cache: bfloat16 [256, 2, 64, 2048], P('seq', None, None, 'tensor'), may hold values from -6 to 6
- task_ids: int32 [256], P('groups'), parts along dimension 0, may hold values from 0 to 255
- cache_lengths: int32 [256], P('groups'), parts along dimension 0, may hold values from 1 to 4096, as said below
- block_table: int32 [256, 32], P('groups'), parts along dimension 0, may hold values from -1 to 255, as said below
Outputs:
- layer_out: bfloat16 [256, 4608], P(('groups', 'seq'), 'tensor'), parts along dimension 0
- fresh_cache: bfloat16 [256, 2, 2048], P(('groups', 'seq'), None, 'tensor'), parts along dimension 0
There are 2 independent parts, one for each index of `groups`. A program takes and returns all parts, laid end to end along the dimension named above; an argument that names none is the same for every part. Nothing has to cross between parts.
Inputs may be any that keep to these rules, and one draw needn't show every extreme that they name: `cache_lengths`: each draw has a request with exactly 4096 cache tokens. block_table[r, j] is the page of cache_pool holding cache tokens j * 128 to (j + 1) * 128 - 1 of request r for j < ceil(cache_lengths[r] / 128), and -1 for the later j; no page is named twice.
All inputs are finite; a program needn't handle non-finite values.
Results may differ from a plain program's by a relative error of at most 0.018.
Values may be sent and summed in bfloat16 or wider, within the bound.
A program may use at most 128 MiB of HBM per device.

v0:
```python
import jax
import jax.numpy as jnp
from jax import lax
from jax.experimental import pallas as pl
from jax.experimental.pallas import tpu as pltpu
from jax.sharding import PartitionSpec as P
import functools
import numpy as np

D = 4608
H = 32
HD = 128


cap_limit = 50.0


def rms_scale(values, gain):
    mean_square = jnp.mean(values * values, axis=-1, keepdims=True)
    return values * lax.rsqrt(mean_square + 1e-06) * gain


def rotate(values, position):
    half_dim = values.shape[-1] // 2
    frequency = 10000.0 ** (-jnp.arange(half_dim, dtype=jnp.float32) / half_dim)
    angles = position.astype(jnp.float32)[:, None] * frequency[None, :]
    cosine = jnp.cos(angles)[:, None, :]
    sines = jnp.sin(angles)[:, None, :]
    first_half = values[..., :half_dim]
    second_half = values[..., half_dim:]
    return jnp.concatenate(
        [first_half * cosine - second_half * sines, second_half * cosine + first_half * sines],
        axis=-1,
    )


def capped(raw_score, score_scale):
    return cap_limit * jnp.tanh(raw_score * score_scale / cap_limit)


def attend(query_block, block, live_mask, score_scale):
    count = block.shape[0]
    length = block.shape[2]
    kv_heads = query_block.shape[1]
    head_dim = query_block.shape[3]
    block_keys = block[:, 0].reshape(count, length, kv_heads, head_dim)
    block_values = block[:, 1].reshape(count, length, kv_heads, head_dim)
    raw_score = jnp.einsum(
        "nkgd,ntkd->nkgt", query_block, block_keys, preferred_element_type=jnp.float32
    )
    weight = jnp.where(live_mask[:, None, None, :], jnp.exp(capped(raw_score, score_scale)), 0.0)
    totals = jnp.sum(weight, axis=-1).reshape(count, -1)
    mixtures = jnp.einsum(
        "nkgt,ntkd->nkgd",
        weight.astype(jnp.bfloat16),
        block_values,
        preferred_element_type=jnp.float32,
    )
    return (totals, mixtures.reshape(count, -1))


def plain_body(
    hidden,
    pre_gain,
    w_query,
    w_key,
    w_value,
    w_out,
    post_gain,
    cache_pool,
    prompt_cache,
    task_ids,
    cache_lengths,
    block_table,
):
    seq_index = lax.axis_index("seq")
    tensor_index = lax.axis_index("tensor")
    own_rows = hidden.shape[0]
    requests = task_ids.shape[0]
    pages_dev = cache_pool.shape[0]
    block_len = cache_pool.shape[2]
    kv_width = cache_pool.shape[3]
    head_dim = HD
    kv_heads = kv_width // head_dim
    query_heads = w_query.shape[1] // head_dim
    group_size = query_heads // kv_heads
    prompt_len = prompt_cache.shape[2]
    tasks_dev = prompt_cache.shape[0]
    score_scale = float(D // H) ** (-0.5)
    first_row = seq_index * own_rows
    own_lengths = lax.dynamic_slice_in_dim(cache_lengths, first_row, own_rows)
    normed = rms_scale(hidden.astype(jnp.float32), pre_gain).astype(jnp.bfloat16)
    position = prompt_len + own_lengths
    query_rows = rotate(
        jnp.dot(normed, w_query, preferred_element_type=jnp.float32).reshape(
            own_rows, query_heads, head_dim
        ),
        position,
    ).astype(jnp.bfloat16)
    key_new = rotate(
        jnp.dot(normed, w_key, preferred_element_type=jnp.float32).reshape(
            own_rows, kv_heads, head_dim
        ),
        position,
    ).astype(jnp.bfloat16)
    value_new = jnp.dot(normed, w_value, preferred_element_type=jnp.float32).astype(jnp.bfloat16)
    fresh_cache = jnp.stack([key_new.reshape(own_rows, kv_width), value_new], axis=1)
    queries = lax.all_gather(
        query_rows.reshape(own_rows, query_heads * head_dim), "seq", axis=0, tiled=True
    )
    page_ids = seq_index * pages_dev + jnp.arange(pages_dev)
    flat_table = block_table.reshape(-1)
    max_blocks = block_table.shape[1]
    matches = flat_table[None, :] == page_ids[:, None]
    entry_index = jnp.arange(flat_table.shape[0])
    page_used = jnp.any(matches, axis=1)
    found_entry = jnp.sum(jnp.where(matches, entry_index[None, :], 0), axis=1)
    page_owner = found_entry // max_blocks
    block_number = found_entry % max_blocks
    owner_hot = (page_owner[:, None] == jnp.arange(requests)[None, :]) & page_used[:, None]
    owner_length = jnp.sum(jnp.where(owner_hot, cache_lengths[None, :], 0), axis=1)
    valid_count = jnp.clip(owner_length - block_number * block_len, 0, block_len)
    page_query = jnp.dot(
        owner_hot.astype(jnp.bfloat16), queries, preferred_element_type=jnp.float32
    ).astype(jnp.bfloat16)
    page_query = page_query.reshape(pages_dev, kv_heads, group_size, head_dim)
    page_live = jnp.arange(block_len)[None, :] < valid_count[:, None]
    page_totals, page_mixtures = attend(page_query, cache_pool, page_live, score_scale)
    spread_hot = owner_hot.astype(jnp.float32).T
    totals = jnp.dot(spread_hot, page_totals, precision=lax.Precision.HIGHEST)
    mixtures = jnp.dot(spread_hot, page_mixtures, precision=lax.Precision.HIGHEST)
    local_task = task_ids - seq_index * tasks_dev
    is_owned = (local_task >= 0) & (local_task < tasks_dev)
    task_rows = prompt_cache[jnp.clip(local_task, 0, tasks_dev - 1)]
    all_query = queries.reshape(requests, kv_heads, group_size, head_dim)
    owned_live = jnp.broadcast_to(is_owned[:, None], (requests, prompt_len))
    prompt_totals, prompt_mixtures = attend(all_query, task_rows, owned_live, score_scale)
    totals = totals + prompt_totals
    mixtures = mixtures + prompt_mixtures
    totals, mixtures = (
        lax.psum_scatter(
            totals.astype(jnp.bfloat16), "seq", scatter_dimension=0, tiled=True
        ).astype(jnp.float32),
        lax.psum_scatter(
            mixtures.astype(jnp.bfloat16), "seq", scatter_dimension=0, tiled=True
        ).astype(jnp.float32),
    )
    own_query = query_rows.reshape(own_rows, kv_heads, group_size, head_dim)
    self_raw = jnp.sum(
        own_query.astype(jnp.float32) * key_new[:, :, None, :].astype(jnp.float32), axis=-1
    )
    self_weight = jnp.exp(capped(self_raw, score_scale))
    rounded = lax.optimization_barrier(self_weight.astype(jnp.bfloat16)).astype(jnp.float32)
    totals = totals + self_weight.reshape(own_rows, -1)
    self_mix = rounded[..., None] * value_new.reshape(own_rows, kv_heads, 1, head_dim).astype(
        jnp.float32
    )
    mixtures = mixtures + self_mix.reshape(own_rows, -1)
    attended = (mixtures.reshape(own_rows, query_heads, head_dim) / totals[..., None]).astype(
        jnp.bfloat16
    )
    projected = jnp.dot(
        attended.reshape(own_rows, query_heads * head_dim),
        w_out,
        preferred_element_type=jnp.float32,
    )
    cols_local = post_gain.shape[0]
    col_start = tensor_index * cols_local
    residual = lax.dynamic_slice_in_dim(hidden, col_start, cols_local, 1).astype(jnp.float32)
    whole_sum = lax.psum(projected.astype(jnp.bfloat16), "tensor").astype(jnp.float32)
    mean_square = jnp.mean(whole_sum * whole_sum, axis=1, keepdims=True)
    scaled = lax.dynamic_slice_in_dim(whole_sum, col_start, cols_local, 1) * lax.rsqrt(
        mean_square + 1e-06
    )
    layer_out = (residual + scaled * post_gain).astype(jnp.bfloat16)
    return (layer_out, fresh_cache)


MESH = pl.DeviceIdType.MESH
VMEM_BYTES = 60 * 1024 * 1024


def greet(axes):
    barrier = pltpu.get_barrier_semaphore()
    amount = 0
    for axis, size in axes:
        me = lax.axis_index(axis)
        for offset in range(1, size):
            peer = lax.rem(me + offset, size)
            pl.semaphore_signal(barrier, inc=1, device_id={axis: peer}, device_id_type=MESH)
            amount += 1
    return barrier, amount


def rope_lanes(x, cosine, sines):
    return x * cosine + pltpu.roll(x, x.shape[-1] // 2, 1) * sines


def project_kernel(
    seq, chunk, prompt_len, lengths, hidden, gain, frequency, w_query, w_key, w_value,
    queries_out, fresh_out,
    normed, gathered, own_query, acc_q, acc_k, acc_v, q_buf, k_buf, v_buf,
    q_sem, k_sem, v_sem, send_sem, recv_sem,
):
    me = lax.axis_index("seq")
    rows, depth = hidden.shape
    steps = depth // chunk
    weights = ((w_query, q_buf, q_sem), (w_key, k_buf, k_sem), (w_value, v_buf, v_sem))

    def copy_of(which, step):
        src, dst, sem = weights[which]
        span = pl.ds(step * chunk, chunk)
        return pltpu.make_async_copy(src.at[span], dst.at[span], sem.at[step])

    for which in range(3):
        for step in range(steps):
            copy_of(which, step).start()
    barrier, amount = greet((("seq", seq),))
    x = hidden[...].astype(jnp.float32)
    mean_square = jnp.mean(x * x, axis=-1, keepdims=True)
    normed[...] = (x * lax.rsqrt(mean_square + 1e-06) * gain[...][None]).astype(jnp.bfloat16)

    def product(which, buf, acc):
        acc[...] = jnp.zeros_like(acc)

        def one(step, carry):
            copy_of(which, step).wait()
            start = pl.multiple_of(step * chunk, chunk)
            acc[...] += jnp.dot(
                normed[:, pl.ds(start, chunk)],
                buf[pl.ds(start, chunk), :],
                preferred_element_type=jnp.float32,
            )
            return carry

        lax.fori_loop(0, steps, one, 0)

    hd = frequency.shape[1]
    row = lax.broadcasted_iota(jnp.int32, (rows, hd), 0)
    position = jnp.zeros((rows, hd), jnp.int32)
    for i in range(rows):
        position = jnp.where(row == i, lengths[me * rows + i] + prompt_len, position)
    angles = position.astype(jnp.float32) * frequency[...]
    lane = lax.broadcasted_iota(jnp.int32, (rows, hd), 1)
    cos_all = jnp.cos(angles)
    sin_all = jnp.sin(angles)
    sin_all = jnp.where(lane < hd // 2, -sin_all, sin_all)
    product(0, q_buf, acc_q)
    for h in range(acc_q.shape[1] // hd):
        lanes = slice(h * hd, (h + 1) * hd)
        own_query[:, lanes] = rope_lanes(acc_q[:, lanes], cos_all, sin_all).astype(jnp.bfloat16)
    pl.semaphore_wait(barrier, amount)
    copies = []
    for offset in range(1, seq):
        peer = lax.rem(me + offset, seq)
        copy = pltpu.make_async_remote_copy(
            src_ref=own_query,
            dst_ref=gathered.at[offset - 1],
            send_sem=send_sem.at[offset - 1],
            recv_sem=recv_sem.at[offset - 1],
            device_id={"seq": peer},
            device_id_type=MESH,
        )
        copy.start()
        copies.append(copy)
    product(1, k_buf, acc_k)
    for h in range(acc_k.shape[1] // hd):
        lanes = slice(h * hd, (h + 1) * hd)
        fresh_out[0, :, lanes] = rope_lanes(acc_k[:, lanes], cos_all, sin_all).astype(jnp.bfloat16)
    product(2, v_buf, acc_v)
    fresh_out[1] = acc_v[...].astype(jnp.bfloat16)
    queries_out[pl.ds(me, 1)] = own_query[...][None]
    for offset in range(1, seq):
        copies[offset - 1].wait()
        source = lax.rem(me + seq - offset, seq)
        queries_out[pl.ds(source, 1)] = gathered[pl.ds(offset - 1, 1)]


def project(seq, prompt_len, lengths, hidden, gain, frequency, w_query, w_key, w_value):
    rows, depth = hidden.shape
    q_width, kv_width = w_query.shape[1], w_key.shape[1]
    chunk = 512 if depth % 512 == 0 else depth
    steps = depth // chunk
    vmem = pl.BlockSpec(memory_space=pltpu.VMEM)
    hbm = pl.BlockSpec(memory_space=pl.ANY)
    return pl.pallas_call(
        functools.partial(project_kernel, seq, chunk, prompt_len),
        out_shape=(
            jax.ShapeDtypeStruct((seq, rows, q_width), jnp.bfloat16),
            jax.ShapeDtypeStruct((2, rows, kv_width), jnp.bfloat16),
        ),
        in_specs=[pl.BlockSpec(memory_space=pltpu.SMEM)] + [vmem] * 3 + [hbm] * 3,
        out_specs=(vmem, vmem),
        scratch_shapes=[
            pltpu.VMEM((rows, depth), jnp.bfloat16),
            pltpu.VMEM((seq - 1, rows, q_width), jnp.bfloat16),
            pltpu.VMEM((rows, q_width), jnp.bfloat16),
            pltpu.VMEM((rows, q_width), jnp.float32),
            pltpu.VMEM((rows, kv_width), jnp.float32),
            pltpu.VMEM((rows, kv_width), jnp.float32),
            pltpu.VMEM((depth, q_width), jnp.bfloat16),
            pltpu.VMEM((depth, kv_width), jnp.bfloat16),
            pltpu.VMEM((depth, kv_width), jnp.bfloat16),
            pltpu.SemaphoreType.DMA((steps,)),
            pltpu.SemaphoreType.DMA((steps,)),
            pltpu.SemaphoreType.DMA((steps,)),
            pltpu.SemaphoreType.DMA((seq - 1,)),
            pltpu.SemaphoreType.DMA((seq - 1,)),
        ],
        compiler_params=pltpu.CompilerParams(
            collective_id=0, has_side_effects=True, vmem_limit_bytes=VMEM_BYTES
        ),
    )(lengths, hidden, gain, frequency, w_query, w_key, w_value)


PAGES = 8
ITEMS = 8


def attend_kernel(
    score_scale, max_blocks, codes, lengths, tasks, queries, fresh, pool, prompts,
    packed, fresh_out,
    fresh_rows, used, q_heads, acc_w, acc_m, pool_buf, prompt_buf, item_req, item_task, pool_sem, prompt_sem,
):
    pages, _, block_len, kv_width = pool.shape
    n_tasks, _, prompt_len, _ = prompts.shape
    requests, heads, hd = q_heads.shape
    kv_heads = kv_width // hd
    group = heads // kv_heads
    seq_index = lax.axis_index("seq")
    batches = pages // PAGES

    def pool_copy(b):
        span = pl.ds(b * PAGES, PAGES)
        return pltpu.make_async_copy(pool.at[span], pool_buf.at[span], pool_sem.at[b])

    def prompt_copy(t):
        return pltpu.make_async_copy(prompts.at[t], prompt_buf.at[t], prompt_sem.at[t])

    for b in range(batches):
        pool_copy(b).start()

    def clear_one(t, carry):
        used[t] = 0
        return carry

    lax.fori_loop(0, n_tasks, clear_one, 0)
    def list_one(r, count):
        local = tasks[r] - seq_index * n_tasks
        owned = (local >= 0) & (local < n_tasks)
        local = jnp.clip(local, 0, n_tasks - 1)
        item_req[count] = r
        item_task[count] = local

        @pl.when(owned & (used[local] == 0))
        def _():
            used[local] = 1
            prompt_copy(local).start()

        return count + jnp.where(owned, 1, 0)

    count = lax.fori_loop(0, requests, list_one, jnp.int32(0))

    for h in range(heads):
        q_heads[:, h, :] = queries[:, h * hd : (h + 1) * hd].astype(jnp.float32)
    acc_w[...] = jnp.zeros_like(acc_w)
    acc_m[...] = jnp.zeros_like(acc_m)
    for i in range(2):
        fresh_rows[:, i, :] = fresh[i].astype(jnp.float32)
    fresh_out[...] = fresh_rows[...].astype(jnp.bfloat16)

    head_of = lax.broadcasted_iota(jnp.int32, (heads, hd), 0) // group
    head_masks = [(head_of == g).astype(jnp.float32) for g in range(kv_heads)]

    def batch(parts):
        raws = []
        for owner, valid, keys, values, length in parts:
            q = q_heads[owner]
            wide = jnp.concatenate([q * m for m in head_masks], axis=1).astype(jnp.bfloat16)
            raws.append(
                lax.dot_general(
                    wide, keys(), (((1,), (1,)), ((), ())), preferred_element_type=jnp.float32
                )
            )
        weights = []
        for raw, (owner, valid, keys, values, length) in zip(raws, parts):
            token = lax.broadcasted_iota(jnp.int32, raw.shape, 1)
            weight = jnp.exp(cap_limit * jnp.tanh(raw * (score_scale / cap_limit)))
            weights.append(jnp.where(token < valid, weight, 0.0))
        mixed = []
        for weight, (owner, valid, keys, values, length) in zip(weights, parts):
            wide = jnp.dot(
                weight.astype(jnp.bfloat16), values(), preferred_element_type=jnp.float32
            )
            mix = wide[:, :hd] * head_masks[0]
            for g in range(1, kv_heads):
                mix += wide[:, g * hd : (g + 1) * hd] * head_masks[g]
            mixed.append(mix)
        for weight, mix, (owner, valid, keys, values, length) in zip(weights, mixed, parts):
            acc_w[owner, :, :length] += weight
            acc_m[owner] += mix

    def page_batch(b, carry):
        pool_copy(b).wait()
        parts = []
        for i in range(PAGES):
            p = b * PAGES + i
            code = codes[p]
            entry = jnp.maximum(code - 1, 0)
            owner = entry // max_blocks
            number = entry - owner * max_blocks
            valid = jnp.where(code > 0, lengths[owner] - number * block_len, 0)
            parts.append(
                (owner, valid, lambda p=p: pool_buf[p, 0], lambda p=p: pool_buf[p, 1], block_len)
            )
        batch(parts)
        return carry

    lax.fori_loop(0, batches, page_batch, 0)

    def wait_one(t, carry):
        @pl.when(used[t] == 1)
        def _():
            prompt_copy(t).wait()

        return carry

    lax.fori_loop(0, n_tasks, wait_one, 0)

    def item_batch(b, carry):
        parts = []
        for i in range(ITEMS):
            j = b * ITEMS + i
            live = j < count
            where = jnp.where(live, j, 0)
            owner = item_req[where]
            t = item_task[where]
            valid = jnp.where(live, prompt_len, 0)
            parts.append(
                (
                    owner, valid, lambda t=t: prompt_buf[t, 0], lambda t=t: prompt_buf[t, 1],
                    prompt_len,
                )
            )
        batch(parts)
        return carry

    lax.fori_loop(0, (count + ITEMS - 1) // ITEMS, item_batch, 0)
    lane = lax.broadcasted_iota(jnp.int32, (requests, hd), 1)
    totals = jnp.zeros((requests, hd), jnp.float32)
    for h in range(heads):
        packed[:, h * hd : (h + 1) * hd] = acc_m[:, h, :].astype(jnp.bfloat16)
        totals = jnp.where(lane == h, jnp.sum(acc_w[:, h, :], axis=1, keepdims=True), totals)
    packed[:, heads * hd :] = totals.astype(jnp.bfloat16)


def attend_local(
    score_scale, max_blocks, codes, lengths, tasks, queries, fresh, pool, prompts, hd
):
    requests, q_width = queries.shape
    heads = q_width // hd
    smem = pl.BlockSpec(memory_space=pltpu.SMEM)
    vmem = pl.BlockSpec(memory_space=pltpu.VMEM)
    hbm = pl.BlockSpec(memory_space=pl.ANY)
    return pl.pallas_call(
        functools.partial(attend_kernel, score_scale, max_blocks),
        out_shape=(
            jax.ShapeDtypeStruct((requests, q_width + hd), jnp.bfloat16),
            jax.ShapeDtypeStruct((fresh.shape[1], 2, fresh.shape[2]), jnp.bfloat16),
        ),
        in_specs=[smem, smem, smem, vmem, vmem, hbm, hbm],
        out_specs=(vmem, vmem),
        scratch_shapes=[
            pltpu.VMEM((fresh.shape[1], 2, fresh.shape[2]), jnp.float32),
            pltpu.SMEM((prompts.shape[0],), jnp.int32),
            pltpu.VMEM((requests, heads, hd), jnp.float32),
            pltpu.VMEM((requests, heads, hd), jnp.float32),
            pltpu.VMEM((requests, heads, hd), jnp.float32),
            pltpu.VMEM(pool.shape, pool.dtype),
            pltpu.VMEM(prompts.shape, prompts.dtype),
            pltpu.SMEM((requests + 1,), jnp.int32),
            pltpu.SMEM((requests + 1,), jnp.int32),
            pltpu.SemaphoreType.DMA((pool.shape[0] // PAGES,)),
            pltpu.SemaphoreType.DMA((prompts.shape[0],)),
        ],
        compiler_params=pltpu.CompilerParams(vmem_limit_bytes=VMEM_BYTES),
    )(codes, lengths, tasks, queries, fresh, pool, prompts)


def output_kernel(
    seq, tensor, score_scale, hd, packed, queries, fresh, gain, w_out,
    out,
    landed, attended, w_buf, sent, arrived, square, squares,
    w_sem, mix_send, mix_recv, part_send, part_recv, square_send, square_recv,
):
    me = lax.axis_index("seq")
    mine = lax.axis_index("tensor")
    rows, cols = out.shape
    order = [(tensor // 2 + i) % tensor for i in range(tensor)]
    order = [o for o in order if o] + [0]

    def w_copy(offset):
        c = lax.rem(mine + offset, tensor)
        start = pl.multiple_of(c * cols, 128)
        return pltpu.make_async_copy(
            w_out.at[:, pl.ds(start, cols)], w_buf.at[offset], w_sem.at[offset]
        )

    barrier, amount = greet((("seq", seq), ("tensor", tensor)))
    for offset in order:
        w_copy(offset).start()
    pl.semaphore_wait(barrier, amount)
    copies = []
    for offset in range(1, seq):
        peer = lax.rem(me + offset, seq)
        copy = pltpu.make_async_remote_copy(
            src_ref=packed.at[peer],
            dst_ref=landed.at[offset - 1],
            send_sem=mix_send.at[offset - 1],
            recv_sem=mix_recv.at[offset - 1],
            device_id={"seq": peer},
            device_id_type=MESH,
        )
        copy.start()
        copies.append(copy)
    q_width = queries.shape[2]
    heads = q_width // hd
    kv_width = fresh.shape[2]
    group = heads // (kv_width // hd)
    self_weights = []
    for h in range(heads):
        g = h // group
        q = queries[me, :, h * hd : (h + 1) * hd].astype(jnp.float32)
        k = fresh[0, :, g * hd : (g + 1) * hd].astype(jnp.float32)
        raw = jnp.sum(q * k, axis=1, keepdims=True)
        self_weights.append(jnp.exp(cap_limit * jnp.tanh(raw * (score_scale / cap_limit))))
    for copy in copies:
        copy.wait()
    for h in range(heads):
        g = h // group
        lanes = slice(h * hd, (h + 1) * hd)
        spot = slice(q_width + h, q_width + h + 1)
        mix = packed[me, :, lanes].astype(jnp.float32)
        total = packed[me, :, q_width:].astype(jnp.float32)
        for s in range(seq - 1):
            mix += landed[s, :, lanes].astype(jnp.float32)
            total += landed[s, :, q_width:].astype(jnp.float32)
        total = total[:, h : h + 1] + self_weights[h]
        rounded = self_weights[h].astype(jnp.bfloat16).astype(jnp.float32)
        mix += rounded * fresh[1, :, g * hd : (g + 1) * hd].astype(jnp.float32)
        attended[:, lanes] = (mix / total).astype(jnp.bfloat16)
    parts = []
    for offset in order:
        w_copy(offset).wait()
        projected = jnp.dot(attended[...], w_buf[offset], preferred_element_type=jnp.float32)
        if offset:
            sent[offset - 1] = projected.astype(jnp.bfloat16)
            copy = pltpu.make_async_remote_copy(
                src_ref=sent.at[offset - 1],
                dst_ref=arrived.at[offset - 1],
                send_sem=part_send.at[offset - 1],
                recv_sem=part_recv.at[offset - 1],
                device_id={"tensor": lax.rem(mine + offset, tensor)},
                device_id_type=MESH,
            )
            copy.start()
            parts.append(copy)
    whole = projected
    for copy in parts:
        copy.wait()
    for s in range(tensor - 1):
        whole += arrived[s].astype(jnp.float32)
    part_square = jnp.sum(whole * whole, axis=1, keepdims=True)
    square[...] = jnp.broadcast_to(part_square, square.shape)
    copies = []
    for offset in range(1, tensor):
        copy = pltpu.make_async_remote_copy(
            src_ref=square,
            dst_ref=squares.at[offset - 1],
            send_sem=square_send.at[offset - 1],
            recv_sem=square_recv.at[offset - 1],
            device_id={"tensor": lax.rem(mine + offset, tensor)},
            device_id_type=MESH,
        )
        copy.start()
        copies.append(copy)
    scaled = whole * gain[...][None]
    for copy in copies:
        copy.wait()
    total_square = square[...]
    for s in range(tensor - 1):
        total_square += squares[s]
    factor = lax.rsqrt(total_square[:, :1] / (cols * tensor) + 1e-06)
    out[...] = scaled * factor


def output_stage(seq, tensor, score_scale, hd, packed, queries, fresh, gain, w_out):
    rows = packed.shape[1]
    cols = gain.shape[0]
    depth = w_out.shape[0]
    vmem = pl.BlockSpec(memory_space=pltpu.VMEM)
    hbm = pl.BlockSpec(memory_space=pl.ANY)
    dma = pltpu.SemaphoreType.DMA
    return pl.pallas_call(
        functools.partial(output_kernel, seq, tensor, score_scale, hd),
        out_shape=jax.ShapeDtypeStruct((rows, cols), jnp.float32),
        in_specs=[vmem] * 4 + [hbm],
        out_specs=vmem,
        scratch_shapes=[
            pltpu.VMEM((seq - 1, rows, packed.shape[2]), jnp.bfloat16),
            pltpu.VMEM((rows, depth), jnp.bfloat16),
            pltpu.VMEM((tensor, depth, cols), jnp.bfloat16),
            pltpu.VMEM((tensor - 1, rows, cols), jnp.bfloat16),
            pltpu.VMEM((tensor - 1, rows, cols), jnp.bfloat16),
            pltpu.VMEM((rows, 128), jnp.float32),
            pltpu.VMEM((tensor - 1, rows, 128), jnp.float32),
            dma((tensor,)),
            dma((seq - 1,)),
            dma((seq - 1,)),
            dma((tensor - 1,)),
            dma((tensor - 1,)),
            dma((tensor - 1,)),
            dma((tensor - 1,)),
        ],
        compiler_params=pltpu.CompilerParams(
            collective_id=1, has_side_effects=True, vmem_limit_bytes=VMEM_BYTES
        ),
    )(packed, queries, fresh, gain, w_out)


def body(
    seq, tensor, hidden, pre_gain, w_query, w_key, w_value, w_out, post_gain,
    cache_pool, prompt_cache, task_ids, cache_lengths, block_table,
):
    seq_index = lax.axis_index("seq")
    own_rows = hidden.shape[0]
    requests = task_ids.shape[0]
    pages_dev = cache_pool.shape[0]
    kv_width = cache_pool.shape[3]
    prompt_len = prompt_cache.shape[2]
    score_scale = float(D // H) ** (-0.5)
    half = HD // 2
    frequency = 10000.0 ** (-np.arange(half) / half)
    frequency = jnp.asarray(np.concatenate([frequency, frequency])[None], jnp.float32)
    queries, fresh = project(
        seq, prompt_len, cache_lengths, hidden, pre_gain, frequency, w_query, w_key, w_value
    )
    queries, fresh, block_table = lax.optimization_barrier((queries, fresh, block_table))
    page_ids = seq_index * pages_dev + jnp.arange(pages_dev)
    flat_table = block_table.reshape(-1)
    matches = flat_table[None, :] == page_ids[:, None]
    entry = jnp.arange(1, flat_table.shape[0] + 1)
    codes = jnp.sum(jnp.where(matches, entry[None, :], 0), axis=1)
    packed, fresh_cache = attend_local(
        score_scale, block_table.shape[1], codes, cache_lengths, task_ids,
        queries.reshape(requests, -1), fresh, cache_pool, prompt_cache, HD,
    )
    update = output_stage(
        seq, tensor, score_scale, HD, packed.reshape(seq, own_rows, -1), queries, fresh,
        post_gain, w_out,
    )
    cols = post_gain.shape[0]
    residual = lax.dynamic_slice_in_dim(hidden, lax.axis_index("tensor") * cols, cols, 1)
    layer_out = (residual.astype(jnp.float32) + update).astype(jnp.bfloat16)
    return (layer_out, fresh_cache)


def solution(mesh):
    seq, tensor = mesh.shape["seq"], mesh.shape["tensor"]

    def chosen(*arrays):
        cols, heads, pages = arrays[6].shape[0], arrays[2].shape[1] // HD, arrays[7].shape[0]
        if cols % 128 or heads % 8 or pages % PAGES or seq < 2 or tensor < 2:
            return plain_body(*arrays)
        return body(seq, tensor, *arrays)

    return jax.shard_map(
        chosen,
        mesh=mesh,
        in_specs=(
            P(("groups", "seq"), None),
            P(),
            P(None, "tensor"),
            P(None, "tensor"),
            P(None, "tensor"),
            P("tensor", None),
            P("tensor"),
            P(("groups", "seq"), None, None, "tensor"),
            P("seq", None, None, "tensor"),
            P("groups"),
            P("groups"),
            P("groups", None),
        ),
        out_specs=(P(("groups", "seq"), "tensor"), P(("groups", "seq"), None, "tensor")),
        check_vma=False,
    )
```

profile of v0, /device:TPU:0, one launch (start us, length us, event | category | flops | bytes accessed | tf_op | source)
XLA Modules:
  0.0 52.4 jit_solution(11487499905112629349)
XLA Ops:
  0.7 0.0 copy-start
  0.7 14.4 %shard_map.140 = (bf16[4,32,1024]{2,1,0:T(8,128)(2,1)}, bf16[2,32,512]{2,1,0:T(8,128)(2,1)}) custom-call(s32[128]{0:T(128)} %lengths.3, bf16[32,4608]{1,0:T(8,128)(2,1)} %hidden.1, f32[4608]{0:T(1024)} %gain.2, f32[1,128]{1,0:T(1,128)} %constant.19.clone.frequency, bf16[4608,1024]{1,0:T(8,128)(2,1)} %w_query.1, bf16[4608,512]{1,0:T(8,128)(2,1)} %w_key.1, ...), custom_call_target="tpu_custom_call" | custom-call | tf_op jit(solution)/shard_map/pallas_call | solution.py:286
  15.0 0.0 copy-done
  15.1 0.1 copy.16
  15.1 0.1 eq.15
  15.2 0.8 %select_reduce_fusion.codes = s32[64]{0:T(128)} fusion(s32[4096]{0:T(1024)S(1)} %iota_add_fusion, s32[4096]{0:T(1024)S(1)} %eq.15, s32[64]{0:T(128)S(1)} %iota_add_fusion.1), kind=kLoop, calls=%fused_computation | loop fusion | flops 786368 | bytes 33280 | tf_op jit(solution)/shard_map/reduce_sum | solution.py:653
  16.0 12.9 %shard_map.141 = (bf16[128,1152]{1,0:T(8,128)(2,1)}, bf16[32,2,512]{2,1,0:T(2,128)(2,1)}) custom-call(s32[64]{0:T(128)} %select_reduce_fusion.codes, s32[128]{0:T(128)} %lengths.3, s32[128]{0:T(128)} %tasks.1, bf16[128,1024]{1,0:T(8,128)(2,1)} %bitcast.2, bf16[2,32,512]{2,1,0:T(8,128)(2,1)} %get-tuple-element.13.fresh, bf16[64,2,128,512]{3,2,1,0:T(8,128)(2,1)} %pool.1, ...), custom_call_target="tpu_custom_call" | custom-call | tf_op jit(solution)/shard_map/pallas_call | solution.py:465
  28.9 21.9 %shard_map.142 = f32[32,1152]{1,0:T(8,128)} custom-call(bf16[4,32,1152]{2,1,0:T(8,128)(2,1)} %bitcast.3, bf16[4,32,1024]{2,1,0:T(8,128)(2,1)} %get-tuple-element.12.queries, bf16[2,32,512]{2,1,0:T(8,128)(2,1)} %get-tuple-element.13.fresh, f32[1152]{0:T(1024)} %gain.3, bf16[1024,4608]{1,0:T(8,128)(2,1)} %w_out.1), custom_call_target="tpu_custom_call" | custom-call | tf_op jit(solution)/shard_map/pallas_call | solution.py:604
  50.8 1.6 %add_convert_fusion = bf16[32,1152]{1,0:T(8,128)(2,1)} fusion(f32[32,1152]{1,0:T(8,128)} %shard_map.142, bf16[32,4608]{1,0:T(8,128)(2,1)} %hidden.1, s32[]{:T(128)S(6)} %select_n.7), kind=kLoop, calls=%fused_computation.1 | loop fusion | flops 110592 | bytes 294916 | tf_op jit(solution)/shard_map/convert_element_type | solution.py:664
  (2 shorter events, 0.0 us)
Async XLA Ops:
  0.7 14.4 %copy-start = (s32[128,32]{0,1:T(8,128)S(1)}, s32[128,32]{0,1:T(8,128)}, u32[]{:S(2)}) copy-start(s32[128,32]{0,1:T(8,128)} %param.24) | copy-start | bytes 49156
where the time goes:
time: 52.7 us; the launch traced here: 52.4 us
  Pallas kernels  49.1 us (93%)
  other arithmetic  2.43 us (5%)
  between operations  0.69 us (1%)
    pallas_call x1, Pallas kernels, output_stage(): pl.pallas_call(functools.partial(output_kernel, seq, tensor, score_scale,...  21.9 us
    pallas_call x1, Pallas kernels, project(): pl.pallas_call(functools.partial(project_kernel, seq, chunk, prompt_len),...  14.4 us
    pallas_call x1, Pallas kernels, attend_local(): pl.pallas_call(functools.partial(attend_kernel, score_scale, max_blocks),...  12.9 us
    convert_element_type x1, other arithmetic, body(): layer_out = (residual.astype(jnp.float32) + update).astype(jnp.bfloat16)  1.61 us

commit v1 on v0

v1 whole, which is shorter than its diff:
```python
import jax
import jax.numpy as jnp
from jax import lax
from jax.experimental import pallas as pl
from jax.experimental.pallas import tpu as pltpu
from jax.sharding import PartitionSpec as P
import functools
import numpy as np

D = 4608
H = 32
HD = 128


cap_limit = 50.0


def rms_scale(values, gain):
    mean_square = jnp.mean(values * values, axis=-1, keepdims=True)
    return values * lax.rsqrt(mean_square + 1e-06) * gain


def rotate(values, position):
    half_dim = values.shape[-1] // 2
    frequency = 10000.0 ** (-jnp.arange(half_dim, dtype=jnp.float32) / half_dim)
    angles = position.astype(jnp.float32)[:, None] * frequency[None, :]
    cosine = jnp.cos(angles)[:, None, :]
    sines = jnp.sin(angles)[:, None, :]
    first_half = values[..., :half_dim]
    second_half = values[..., half_dim:]
    return jnp.concatenate(
        [first_half * cosine - second_half * sines, second_half * cosine + first_half * sines],
        axis=-1,
    )


def capped(raw_score, score_scale):
    return cap_limit * jnp.tanh(raw_score * score_scale / cap_limit)


def attend(query_block, block, live_mask, score_scale):
    count = block.shape[0]
    length = block.shape[2]
    kv_heads = query_block.shape[1]
    head_dim = query_block.shape[3]
    block_keys = block[:, 0].reshape(count, length, kv_heads, head_dim)
    block_values = block[:, 1].reshape(count, length, kv_heads, head_dim)
    raw_score = jnp.einsum(
        "nkgd,ntkd->nkgt", query_block, block_keys, preferred_element_type=jnp.float32
    )
    weight = jnp.where(live_mask[:, None, None, :], jnp.exp(capped(raw_score, score_scale)), 0.0)
    totals = jnp.sum(weight, axis=-1).reshape(count, -1)
    mixtures = jnp.einsum(
        "nkgt,ntkd->nkgd",
        weight.astype(jnp.bfloat16),
        block_values,
        preferred_element_type=jnp.float32,
    )
    return (totals, mixtures.reshape(count, -1))


def plain_body(
    hidden,
    pre_gain,
    w_query,
    w_key,
    w_value,
    w_out,
    post_gain,
    cache_pool,
    prompt_cache,
    task_ids,
    cache_lengths,
    block_table,
):
    seq_index = lax.axis_index("seq")
    tensor_index = lax.axis_index("tensor")
    own_rows = hidden.shape[0]
    requests = task_ids.shape[0]
    pages_dev = cache_pool.shape[0]
    block_len = cache_pool.shape[2]
    kv_width = cache_pool.shape[3]
    head_dim = HD
    kv_heads = kv_width // head_dim
    query_heads = w_query.shape[1] // head_dim
    group_size = query_heads // kv_heads
    prompt_len = prompt_cache.shape[2]
    tasks_dev = prompt_cache.shape[0]
    score_scale = float(D // H) ** (-0.5)
    first_row = seq_index * own_rows
    own_lengths = lax.dynamic_slice_in_dim(cache_lengths, first_row, own_rows)
    normed = rms_scale(hidden.astype(jnp.float32), pre_gain).astype(jnp.bfloat16)
    position = prompt_len + own_lengths
    query_rows = rotate(
        jnp.dot(normed, w_query, preferred_element_type=jnp.float32).reshape(
            own_rows, query_heads, head_dim
        ),
        position,
    ).astype(jnp.bfloat16)
    key_new = rotate(
        jnp.dot(normed, w_key, preferred_element_type=jnp.float32).reshape(
            own_rows, kv_heads, head_dim
        ),
        position,
    ).astype(jnp.bfloat16)
    value_new = jnp.dot(normed, w_value, preferred_element_type=jnp.float32).astype(jnp.bfloat16)
    fresh_cache = jnp.stack([key_new.reshape(own_rows, kv_width), value_new], axis=1)
    queries = lax.all_gather(
        query_rows.reshape(own_rows, query_heads * head_dim), "seq", axis=0, tiled=True
    )
    page_ids = seq_index * pages_dev + jnp.arange(pages_dev)
    flat_table = block_table.reshape(-1)
    max_blocks = block_table.shape[1]
    matches = flat_table[None, :] == page_ids[:, None]
    entry_index = jnp.arange(flat_table.shape[0])
    page_used = jnp.any(matches, axis=1)
    found_entry = jnp.sum(jnp.where(matches, entry_index[None, :], 0), axis=1)
    page_owner = found_entry // max_blocks
    block_number = found_entry % max_blocks
    owner_hot = (page_owner[:, None] == jnp.arange(requests)[None, :]) & page_used[:, None]
    owner_length = jnp.sum(jnp.where(owner_hot, cache_lengths[None, :], 0), axis=1)
    valid_count = jnp.clip(owner_length - block_number * block_len, 0, block_len)
    page_query = jnp.dot(
        owner_hot.astype(jnp.bfloat16), queries, preferred_element_type=jnp.float32
    ).astype(jnp.bfloat16)
    page_query = page_query.reshape(pages_dev, kv_heads, group_size, head_dim)
    page_live = jnp.arange(block_len)[None, :] < valid_count[:, None]
    page_totals, page_mixtures = attend(page_query, cache_pool, page_live, score_scale)
    spread_hot = owner_hot.astype(jnp.float32).T
    totals = jnp.dot(spread_hot, page_totals, precision=lax.Precision.HIGHEST)
    mixtures = jnp.dot(spread_hot, page_mixtures, precision=lax.Precision.HIGHEST)
    local_task = task_ids - seq_index * tasks_dev
    is_owned = (local_task >= 0) & (local_task < tasks_dev)
    task_rows = prompt_cache[jnp.clip(local_task, 0, tasks_dev - 1)]
    all_query = queries.reshape(requests, kv_heads, group_size, head_dim)
    owned_live = jnp.broadcast_to(is_owned[:, None], (requests, prompt_len))
    prompt_totals, prompt_mixtures = attend(all_query, task_rows, owned_live, score_scale)
    totals = totals + prompt_totals
    mixtures = mixtures + prompt_mixtures
    totals, mixtures = (
        lax.psum_scatter(
            totals.astype(jnp.bfloat16), "seq", scatter_dimension=0, tiled=True
        ).astype(jnp.float32),
        lax.psum_scatter(
            mixtures.astype(jnp.bfloat16), "seq", scatter_dimension=0, tiled=True
        ).astype(jnp.float32),
    )
    own_query = query_rows.reshape(own_rows, kv_heads, group_size, head_dim)
    self_raw = jnp.sum(
        own_query.astype(jnp.float32) * key_new[:, :, None, :].astype(jnp.float32), axis=-1
    )
    self_weight = jnp.exp(capped(self_raw, score_scale))
    rounded = lax.optimization_barrier(self_weight.astype(jnp.bfloat16)).astype(jnp.float32)
    totals = totals + self_weight.reshape(own_rows, -1)
    self_mix = rounded[..., None] * value_new.reshape(own_rows, kv_heads, 1, head_dim).astype(
        jnp.float32
    )
    mixtures = mixtures + self_mix.reshape(own_rows, -1)
    attended = (mixtures.reshape(own_rows, query_heads, head_dim) / totals[..., None]).astype(
        jnp.bfloat16
    )
    projected = jnp.dot(
        attended.reshape(own_rows, query_heads * head_dim),
        w_out,
        preferred_element_type=jnp.float32,
    )
    cols_local = post_gain.shape[0]
    col_start = tensor_index * cols_local
    residual = lax.dynamic_slice_in_dim(hidden, col_start, cols_local, 1).astype(jnp.float32)
    whole_sum = lax.psum(projected.astype(jnp.bfloat16), "tensor").astype(jnp.float32)
    mean_square = jnp.mean(whole_sum * whole_sum, axis=1, keepdims=True)
    scaled = lax.dynamic_slice_in_dim(whole_sum, col_start, cols_local, 1) * lax.rsqrt(
        mean_square + 1e-06
    )
    layer_out = (residual + scaled * post_gain).astype(jnp.bfloat16)
    return (layer_out, fresh_cache)


MESH = pl.DeviceIdType.MESH
VMEM_BYTES = 62 * 1024 * 1024


def rope_lanes(x, cosine, sines):
    return x * cosine + pltpu.roll(x, x.shape[-1] // 2, 1) * sines


SLOTS = 16
TOKENS = 128


def attend_groups(groups, heads, kv_heads, hd, score_scale):
    tiles = kv_heads * hd // 256
    tile_heads = heads // tiles
    rows = tile_heads * SLOTS
    slot = lax.broadcasted_iota(jnp.int32, (SLOTS, TOKENS), 0)

    def stacked(x):
        return jnp.concatenate([x] * tile_heads, axis=0)

    scores = []
    for qwide, keys, values, pairs, per, live in groups:
        unit = stacked(slot // per)
        chosen = [None] * tiles
        for pair in range(pairs):
            for t in range(tiles):
                raw = lax.dot_general(
                    qwide[t * rows : (t + 1) * rows, t * 256 : (t + 1) * 256],
                    keys(pair, t),
                    (((1,), (1,)), ((), ())),
                    preferred_element_type=jnp.float32,
                )
                for u in range(2):
                    part = raw[:, u * TOKENS : (u + 1) * TOKENS]
                    if chosen[t] is None:
                        chosen[t] = part
                    else:
                        chosen[t] = jnp.where(unit == 2 * pair + u, part, chosen[t])
        scores.append(chosen)
    results = []
    for chosen, (qwide, keys, values, pairs, per, live) in zip(scores, groups):
        wide_live = stacked(live)
        mixes, totals = [], []
        for t in range(tiles):
            weight = jnp.exp(cap_limit * jnp.tanh(chosen[t] * (score_scale / cap_limit)))
            weight = jnp.where(wide_live > 0, weight, 0.0)
            total = jnp.sum(weight, axis=1, keepdims=True)
            narrow = weight.astype(jnp.bfloat16)
            acc = None
            for pair in range(pairs):
                pieces = []
                for u in range(2):
                    keep = (slot // per == 2 * pair + u).astype(jnp.float32).astype(jnp.bfloat16)
                    pieces.append(narrow * stacked(keep))
                term = jnp.dot(
                    jnp.concatenate(pieces, axis=1),
                    values(pair, t),
                    preferred_element_type=jnp.float32,
                )
                acc = term if acc is None else acc + term
            group = heads // kv_heads
            for i in range(tile_heads):
                span = slice(i * SLOTS, (i + 1) * SLOTS)
                kv = i // group
                mixes.append(acc[span, kv * hd : (kv + 1) * hd])
                totals.append(total[span])
        lane = lax.broadcasted_iota(jnp.int32, (SLOTS, hd), 1)
        packed_total = jnp.zeros((SLOTS, hd), jnp.float32)
        for h in range(heads):
            packed_total = jnp.where(lane == h, totals[h], packed_total)
        results.append(mixes + [packed_total])
    return results


def layer_kernel(
    seq, tensor, score_scale, hd, steps,
    lengths_in, tasks_in, tasks_row_in, table_in, hidden_in, pre_gain_in, frequency_in, post_gain_in,
    w_query, w_key, w_value, w_out, pool, prompts,
    out, fresh_out,
    lengths, tasks, tasks_row, table, hidden, pre_gain, frequency, post_gain,
    normed, queries, q_buf, k_buf, v_buf, w_buf, pool_buf, prompt_buf,
    onehot, onehot_t, valid, owned, page_query, qwide, page_mix, both, req_mix, packed, landed,
    fresh, fresh_rows, attended, sent, arrived, square, squares,
    small_sem, q_sem, k_sem, v_sem, w_sem, pool_sem, prompt_sem,
    query_send, query_recv, mix_send, mix_recv, part_send, part_recv, square_send, square_recv,
):
    me = lax.axis_index("seq")
    mine = lax.axis_index("tensor")
    rows, depth = hidden.shape
    cols = out.shape[1]
    requests = lengths.shape[1]
    q_width = q_buf.shape[1]
    kv_width = k_buf.shape[1]
    heads, kv_heads = q_width // hd, kv_width // hd
    group = heads // kv_heads
    pages, _, block_len, _ = pool.shape
    n_tasks, _, prompt_len, _ = prompts.shape
    max_blocks = table.shape[0]
    half = q_width // 2
    chunk = depth // steps

    smalls = []
    for i, (src, dst) in enumerate((
        (hidden_in, hidden), (pre_gain_in, pre_gain), (frequency_in, frequency),
        (lengths_in, lengths), (tasks_in, tasks), (tasks_row_in, tasks_row),
        (table_in, table), (post_gain_in, post_gain),
    )):
        smalls.append(pltpu.make_async_copy(src, dst, small_sem.at[i]))

    def q_copy(n, c):
        span, lanes = pl.ds(c * chunk, chunk), pl.ds(n * half, half)
        return pltpu.make_async_copy(
            w_query.at[span, lanes], q_buf.at[span, lanes], q_sem.at[n * steps + c]
        )

    def kv_copy(src, dst, sem, c):
        span = pl.ds(c * chunk, chunk)
        return pltpu.make_async_copy(src.at[span], dst.at[span], sem.at[c])

    def pool_copy(b):
        span = pl.ds(b * SLOTS, SLOTS)
        return pltpu.make_async_copy(pool.at[span], pool_buf.at[span], pool_sem.at[b])

    def prompt_copy(b):
        span = pl.ds(b * SLOTS, SLOTS)
        return pltpu.make_async_copy(prompts.at[span], prompt_buf.at[span], prompt_sem.at[b])

    def partners(i):
        return [3 - i, lax.rem(i + 2, 4), i + 1 - 2 * lax.rem(i, 2)]

    seq_peers = partners(me)
    tensor_peers = partners(mine)

    def w_copy(k):
        column = tensor_peers[k] if k < 3 else mine
        start = pl.multiple_of(column * cols, 128)
        return pltpu.make_async_copy(w_out.at[:, pl.ds(start, cols)], w_buf.at[k], w_sem.at[k])

    smalls[0].start()
    smalls[1].start()
    for n in range(2):
        for c in range(steps):
            q_copy(n, c).start()
        if n == 0:
            for copy in smalls[2:]:
                copy.start()
    for b in range(pages // SLOTS):
        pool_copy(b).start()
    for b in range(n_tasks // SLOTS):
        prompt_copy(b).start()
    for c in range(steps):
        kv_copy(w_key, k_buf, k_sem, c).start()
        kv_copy(w_value, v_buf, v_sem, c).start()
    for k in range(4):
        w_copy(k).start()

    barrier = pltpu.get_barrier_semaphore()
    for peer in seq_peers:
        pl.semaphore_signal(barrier, inc=1, device_id={"seq": peer}, device_id_type=MESH)
    for peer in tensor_peers:
        pl.semaphore_signal(barrier, inc=1, device_id={"tensor": peer}, device_id_type=MESH)

    qwide[...] = jnp.zeros_like(qwide)
    for copy in smalls:
        copy.wait()
    x = hidden[...].astype(jnp.float32)
    mean_square = jnp.mean(x * x, axis=-1, keepdims=True)
    normed[...] = (x * lax.rsqrt(mean_square + 1e-06) * pre_gain[...][None]).astype(jnp.bfloat16)

    row = lax.broadcasted_iota(jnp.int32, (rows, requests), 0)
    column = lax.broadcasted_iota(jnp.int32, (rows, requests), 1)
    own_length = jnp.sum(
        jnp.where(column == me * rows + row, lengths[...].astype(jnp.float32), 0.0),
        axis=1, keepdims=True,
    )
    angles = (own_length + prompt_len) * frequency[...]
    lane = lax.broadcasted_iota(jnp.int32, (rows, hd), 1)
    cos_all = jnp.cos(angles)
    sin_all = jnp.sin(angles)
    sin_all = jnp.where(lane < hd // 2, -sin_all, sin_all)

    query_copies = []
    for n in range(2):
        lanes = slice(n * half, (n + 1) * half)
        acc = None
        for c in range(steps):
            q_copy(n, c).wait()
            term = jnp.dot(
                normed[:, c * chunk : (c + 1) * chunk],
                q_buf[c * chunk : (c + 1) * chunk, lanes],
                preferred_element_type=jnp.float32,
            )
            acc = term if acc is None else acc + term
        turned = jnp.concatenate(
            [
                rope_lanes(acc[:, i * hd : (i + 1) * hd], cos_all, sin_all)
                for i in range(half // hd)
            ],
            axis=1,
        ).astype(jnp.bfloat16)
        queries[pl.ds(me, 1), :, lanes] = turned[None]
        if n == 0:
            pl.semaphore_wait(barrier, 6)
        for k, peer in enumerate(seq_peers):
            where = queries.at[me, :, pl.ds(n * half, half)]
            copy = pltpu.make_async_remote_copy(
                src_ref=where, dst_ref=where,
                send_sem=query_send.at[n * 3 + k], recv_sem=query_recv.at[n * 3 + k],
                device_id={"seq": peer}, device_id_type=MESH,
            )
            copy.start()
            query_copies.append(copy)

    page_id = me * pages + lax.broadcasted_iota(jnp.int32, (pages, requests), 0)

    def match_one(j, carry):
        hot, count = carry
        hit = jnp.broadcast_to(table[pl.ds(j, 1), :], (pages, requests)) == page_id
        tokens = jnp.broadcast_to(
            jnp.clip(lengths[...] - j * block_len, 0, block_len), (pages, requests)
        )
        return jnp.where(hit, 1.0, hot), jnp.where(hit, tokens.astype(jnp.float32), count)

    zeros = jnp.zeros((pages, requests), jnp.float32)
    hot, count = lax.fori_loop(0, max_blocks, match_one, (zeros, zeros))
    onehot[...] = hot.astype(jnp.bfloat16)
    turned = hot.T.astype(jnp.bfloat16)
    onehot_t[...] = jnp.concatenate([turned, turned], axis=1)
    valid[...] = jnp.broadcast_to(jnp.sum(count, axis=1, keepdims=True), valid.shape)
    line = lax.broadcasted_iota(jnp.int32, (requests, requests), 0)
    across = lax.broadcasted_iota(jnp.int32, (requests, requests), 1)
    local = tasks_row[...] - me * n_tasks
    is_owned = jnp.where((local >= 0) & (local < n_tasks), 1.0, 0.0)
    owned[...] = jnp.broadcast_to(
        jnp.sum(jnp.where(line == across, is_owned, 0.0), axis=1, keepdims=True), owned.shape
    )

    for copy in query_copies:
        copy.wait()
    all_queries = queries[...].reshape(requests, q_width)
    page_query[...] = jnp.dot(
        onehot[...], all_queries, preferred_element_type=jnp.float32
    ).astype(jnp.bfloat16)

    def widen(slot, source):
        for h in range(heads):
            kv = h // group
            qwide[slot, h * SLOTS : (h + 1) * SLOTS, kv * hd : (kv + 1) * hd] = source(
                slice(h * hd, (h + 1) * hd)
            )

    token = lax.broadcasted_iota(jnp.int32, (SLOTS, TOKENS), 1)

    def pool_step(step, carry):
        groups = []
        starts = []
        for s in range(2):
            g = step * 2 + s
            pool_copy(g).wait()
            start = pl.multiple_of(g * SLOTS, SLOTS)
            widen(s, lambda lanes, start=start: page_query[pl.ds(start, SLOTS), lanes])

            def load(which, start=start):
                def one(pair, t):
                    return pool_buf[
                        pl.ds(start + 2 * pair, 2), which, :, t * 256 : (t + 1) * 256
                    ].reshape(2 * block_len, 256)

                return one

            live = jnp.where(
                token.astype(jnp.float32) < valid[pl.ds(start, SLOTS), :], 1.0, 0.0
            )
            groups.append((qwide.at[s], load(0), load(1), SLOTS // 2, 1, live))
            starts.append(start)
        for start, result in zip(
            starts, attend_groups(groups, heads, kv_heads, hd, score_scale)
        ):
            for i, piece in enumerate(result):
                page_mix[pl.ds(start, SLOTS), i * hd : (i + 1) * hd] = piece
        return carry

    lax.fori_loop(0, pages // (2 * SLOTS), pool_step, 0)
    high = page_mix[...].astype(jnp.bfloat16)
    both[:pages, :] = high
    both[pages:, :] = (page_mix[...] - high.astype(jnp.float32)).astype(jnp.bfloat16)
    req_mix[...] = jnp.dot(onehot_t[...], both[...], preferred_element_type=jnp.float32)

    for b in range(n_tasks // SLOTS):
        prompt_copy(b).wait()
    per = TOKENS // prompt_len
    slot_of = lax.broadcasted_iota(jnp.int32, (SLOTS, TOKENS), 0)
    fits = token // prompt_len == slot_of % per
    mix_copies = []
    for k, peer in enumerate(seq_peers + [me]):
        groups = []
        for s in range(rows // SLOTS):
            first = peer * rows + s * SLOTS
            widen(s, lambda lanes, s=s: queries[peer, s * SLOTS : (s + 1) * SLOTS, lanes])
            places = [
                jnp.clip(tasks[first + i] - me * n_tasks, 0, n_tasks - 1) for i in range(SLOTS)
            ]

            def load(which, places=places):
                def one(pair, t):
                    return jnp.concatenate(
                        [
                            prompt_buf[place, which, :, t * 256 : (t + 1) * 256]
                            for place in places[pair * 2 * per : (pair + 1) * 2 * per]
                        ],
                        axis=0,
                    )

                return one

            start = pl.multiple_of(first, SLOTS)
            live = jnp.where(fits, owned[pl.ds(start, SLOTS), :], 0.0)
            groups.append((qwide.at[s], load(0), load(1), SLOTS // (2 * per), per, live))
        for s, result in enumerate(attend_groups(groups, heads, kv_heads, hd, score_scale)):
            start = pl.multiple_of(peer * rows + s * SLOTS, SLOTS)
            for i, piece in enumerate(result):
                lanes = slice(i * hd, (i + 1) * hd)
                sums = req_mix[pl.ds(start, SLOTS), lanes] + piece
                if k < 3:
                    packed[k, s * SLOTS : (s + 1) * SLOTS, lanes] = sums.astype(jnp.bfloat16)
                else:
                    req_mix[pl.ds(start, SLOTS), lanes] = sums
        if k < 3:
            copy = pltpu.make_async_remote_copy(
                src_ref=packed.at[k], dst_ref=landed.at[k],
                send_sem=mix_send.at[k], recv_sem=mix_recv.at[k],
                device_id={"seq": peer}, device_id_type=MESH,
            )
            copy.start()
            mix_copies.append(copy)

    kv_new = []
    for src, dst, sem in ((w_key, k_buf, k_sem), (w_value, v_buf, v_sem)):
        acc = None
        for c in range(steps):
            kv_copy(src, dst, sem, c).wait()
            term = jnp.dot(
                normed[:, c * chunk : (c + 1) * chunk],
                dst[c * chunk : (c + 1) * chunk, :],
                preferred_element_type=jnp.float32,
            )
            acc = term if acc is None else acc + term
        kv_new.append(acc)
    for g in range(kv_heads):
        lanes = slice(g * hd, (g + 1) * hd)
        fresh[0, :, lanes] = rope_lanes(kv_new[0][:, lanes], cos_all, sin_all).astype(jnp.bfloat16)
    fresh[1] = kv_new[1].astype(jnp.bfloat16)
    for i in range(2):
        fresh_rows[:, i, :] = fresh[i].astype(jnp.float32)
    fresh_out[...] = fresh_rows[...].astype(jnp.bfloat16)
    self_weights = []
    for h in range(heads):
        g = h // group
        q = queries[me, :, h * hd : (h + 1) * hd].astype(jnp.float32)
        k = fresh[0, :, g * hd : (g + 1) * hd].astype(jnp.float32)
        raw = jnp.sum(q * k, axis=1, keepdims=True)
        self_weights.append(jnp.exp(cap_limit * jnp.tanh(raw * (score_scale / cap_limit))))
    for copy in mix_copies:
        copy.wait()
    own = pl.ds(pl.multiple_of(me * rows, SLOTS), rows)
    totals = req_mix[own, q_width:]
    for k in range(3):
        totals += landed[k, :, q_width:].astype(jnp.float32)
    for h in range(heads):
        g = h // group
        lanes = slice(h * hd, (h + 1) * hd)
        mix = req_mix[own, lanes]
        for k in range(3):
            mix += landed[k, :, lanes].astype(jnp.float32)
        total = totals[:, h : h + 1] + self_weights[h]
        rounded = self_weights[h].astype(jnp.bfloat16).astype(jnp.float32)
        mix += rounded * fresh[1, :, g * hd : (g + 1) * hd].astype(jnp.float32)
        attended[:, lanes] = (mix / total).astype(jnp.bfloat16)

    parts = []
    for k in range(4):
        w_copy(k).wait()
        projected = jnp.dot(attended[...], w_buf[k], preferred_element_type=jnp.float32)
        if k < 3:
            sent[k] = projected.astype(jnp.bfloat16)
            copy = pltpu.make_async_remote_copy(
                src_ref=sent.at[k], dst_ref=arrived.at[k],
                send_sem=part_send.at[k], recv_sem=part_recv.at[k],
                device_id={"tensor": tensor_peers[k]}, device_id_type=MESH,
            )
            copy.start()
            parts.append(copy)
    whole = projected
    for k in (2, 0, 1):
        parts[k].wait()
        whole += arrived[k].astype(jnp.float32)
    part_square = jnp.sum(whole * whole, axis=1, keepdims=True)
    row = lax.broadcasted_iota(jnp.int32, (rows, 128), 0)
    diagonal = row == lax.broadcasted_iota(jnp.int32, (rows, 128), 1)
    square[...] = jnp.sum(jnp.where(diagonal, part_square, 0.0), axis=0, keepdims=True)
    copies = []
    for k, peer in enumerate(tensor_peers):
        copy = pltpu.make_async_remote_copy(
            src_ref=square, dst_ref=squares.at[k],
            send_sem=square_send.at[k], recv_sem=square_recv.at[k],
            device_id={"tensor": peer}, device_id_type=MESH,
        )
        copy.start()
        copies.append(copy)
    scaled = whole * post_gain[...][None]
    start = pl.multiple_of(mine * cols, 128)
    residual = hidden[:, pl.ds(start, cols)].astype(jnp.float32)
    for copy in copies:
        copy.wait()
    total_square = square[...]
    for k in range(3):
        total_square += squares[k]
    column_square = jnp.sum(jnp.where(diagonal, total_square, 0.0), axis=1, keepdims=True)
    factor = lax.rsqrt(column_square / (cols * tensor) + 1e-06)
    out[...] = (residual + scaled * factor).astype(jnp.bfloat16)


STEPS = 3


def body(
    seq, tensor, hidden, pre_gain, w_query, w_key, w_value, w_out, post_gain,
    cache_pool, prompt_cache, task_ids, cache_lengths, block_table,
):
    rows, depth = hidden.shape
    requests = task_ids.shape[0]
    pages, _, _, kv_width = cache_pool.shape
    n_tasks = prompt_cache.shape[0]
    q_width = w_query.shape[1]
    heads = q_width // HD
    cols = post_gain.shape[0]
    score_scale = float(D // H) ** (-0.5)
    half = HD // 2
    frequency = 10000.0 ** (-np.arange(half) / half)
    frequency = jnp.asarray(np.concatenate([frequency, frequency])[None], jnp.float32)
    vmem = pl.BlockSpec(memory_space=pltpu.VMEM)
    hbm = pl.BlockSpec(memory_space=pl.ANY)
    dma = pltpu.SemaphoreType.DMA
    bf16, f32, i32 = jnp.bfloat16, jnp.float32, jnp.int32
    packed_width = q_width + HD
    return pl.pallas_call(
        functools.partial(layer_kernel, seq, tensor, score_scale, HD, STEPS),
        out_shape=(
            jax.ShapeDtypeStruct((rows, cols), bf16),
            jax.ShapeDtypeStruct((rows, 2, kv_width), bf16),
        ),
        in_specs=[hbm] * 14,
        out_specs=(vmem, vmem),
        scratch_shapes=[
            pltpu.VMEM((1, requests), i32),
            pltpu.SMEM((requests,), i32),
            pltpu.VMEM((1, requests), i32),
            pltpu.VMEM((block_table.shape[1], requests), i32),
            pltpu.VMEM((rows, depth), bf16),
            pltpu.VMEM((depth,), f32),
            pltpu.VMEM((1, HD), f32),
            pltpu.VMEM((cols,), f32),
            pltpu.VMEM((rows, depth), bf16),
            pltpu.VMEM((seq, rows, q_width), bf16),
            pltpu.VMEM((depth, q_width), bf16),
            pltpu.VMEM((depth, kv_width), bf16),
            pltpu.VMEM((depth, kv_width), bf16),
            pltpu.VMEM((tensor, w_out.shape[0], cols), bf16),
            pltpu.VMEM(cache_pool.shape, bf16),
            pltpu.VMEM(prompt_cache.shape, bf16),
            pltpu.VMEM((pages, requests), bf16),
            pltpu.VMEM((requests, 2 * pages), bf16),
            pltpu.VMEM((pages, TOKENS), f32),
            pltpu.VMEM((requests, TOKENS), f32),
            pltpu.VMEM((pages, q_width), bf16),
            pltpu.VMEM((2, heads * SLOTS, kv_width), bf16),
            pltpu.VMEM((pages, packed_width), f32),
            pltpu.VMEM((2 * pages, packed_width), bf16),
            pltpu.VMEM((requests, packed_width), f32),
            pltpu.VMEM((3, rows, packed_width), bf16),
            pltpu.VMEM((3, rows, packed_width), bf16),
            pltpu.VMEM((2, rows, kv_width), bf16),
            pltpu.VMEM((rows, 2, kv_width), f32),
            pltpu.VMEM((rows, q_width), bf16),
            pltpu.VMEM((3, rows, cols), bf16),
            pltpu.VMEM((3, rows, cols), bf16),
            pltpu.VMEM((1, 128), f32),
            pltpu.VMEM((3, 1, 128), f32),
            dma((8,)),
            dma((2 * STEPS,)),
            dma((STEPS,)),
            dma((STEPS,)),
            dma((tensor,)),
            dma((pages // SLOTS,)),
            dma((n_tasks // SLOTS,)),
            dma((6,)),
            dma((6,)),
            dma((3,)),
            dma((3,)),
            dma((3,)),
            dma((3,)),
            dma((3,)),
            dma((3,)),
        ],
        compiler_params=pltpu.CompilerParams(
            collective_id=0, has_side_effects=True, vmem_limit_bytes=VMEM_BYTES
        ),
    )(
        cache_lengths.reshape(1, -1), task_ids, task_ids.reshape(1, -1), block_table.T,
        hidden, pre_gain, frequency, post_gain,
        w_query, w_key, w_value, w_out, cache_pool, prompt_cache,
    )


def fits(seq, tensor, arrays):
    hidden, w_query, w_key, post_gain = arrays[0], arrays[2], arrays[3], arrays[6]
    pool, prompts, tasks = arrays[7], arrays[8], arrays[9]
    return (
        seq == 4
        and tensor == 4
        and hidden.shape[0] == 2 * SLOTS
        and hidden.shape[1] % (STEPS * 256) == 0
        and w_query.shape[1] % 256 == 0
        and w_key.shape[1] % 256 == 0
        and w_query.shape[1] % w_key.shape[1] == 0
        and post_gain.shape[0] % 128 == 0
        and pool.shape[0] == 64
        and pool.shape[2] == TOKENS
        and prompts.shape[0] % SLOTS == 0
        and prompts.shape[2] == TOKENS // 2
        and tasks.shape[0] == 128
    )


def solution(mesh):
    seq, tensor = mesh.shape["seq"], mesh.shape["tensor"]

    def chosen(*arrays):
        if not fits(seq, tensor, arrays):
            return plain_body(*arrays)
        return body(seq, tensor, *arrays)

    return jax.shard_map(
        chosen,
        mesh=mesh,
        in_specs=(
            P(("groups", "seq"), None),
            P(),
            P(None, "tensor"),
            P(None, "tensor"),
            P(None, "tensor"),
            P("tensor", None),
            P("tensor"),
            P(("groups", "seq"), None, None, "tensor"),
            P("seq", None, None, "tensor"),
            P("groups"),
            P("groups"),
            P("groups", None),
        ),
        out_specs=(P(("groups", "seq"), "tensor"), P(("groups", "seq"), None, "tensor")),
        check_vma=False,
    )
```

time: 52.7 us -> 50 us (0.949)
  Pallas kernels: 49.1 us -> 46.2 us
  local copies, waits for them, and re-layouts: 0.18 us -> 3.04 us
  other arithmetic: 2.43 us -> 0 us
    unnamed x2, local copies, waits for them, and re-layouts: 0.01 us -> 3.04 us
    pallas_call x3 -> x1, Pallas kernels: 49.1 us -> 46.2 us  [body(): pl.pallas_call(functools.partial(layer_kernel, seq, tensor, score_scale,...]
    convert_element_type x1 -> x0, other arithmetic: 1.61 us -> none  [body(): layer_out = (residual.astype(jnp.float32) + update).astype(jnp.bfloat16)]
    reduce_sum x1 -> x0, other arithmetic: 0.8 us -> none  [body(): codes = jnp.sum(jnp.where(matches, entry[None, :], 0), axis=1)]
where the time goes in v1:
time: 50 us; the launch traced here: 49.8 us
  Pallas kernels  46.2 us (92%)
  local copies, waits for them, and re-layouts  3.04 us (6%)
  between operations  0.64 us (1%)
    pallas_call x1, Pallas kernels, body(): pl.pallas_call(functools.partial(layer_kernel, seq, tensor, score_scale,...  46.2 us
    unnamed x2, local copies, waits for them, and re-layouts  3.04 us

profile of v1, /device:TPU:0, one launch (start us, length us, event | category | flops | bytes accessed | tf_op | source)
XLA Modules:
  0.0 49.8 jit_solution(10351556802651918352)
XLA Ops:
  0.6 46.2 %shard_map.140 = (bf16[32,1152]{1,0:T(8,128)(2,1)}, bf16[32,2,512]{2,1,0:T(2,128)(2,1)}) custom-call(s32[1,128]{1,0:T(1,128)} %bitcast.5, s32[128]{0:T(128)} %tasks_in.1, s32[1,128]{1,0:T(1,128)} %bitcast.4, s32[32,128]{1,0:T(8,128)} %bitcast.3, bf16[32,4608]{1,0:T(8,128)(2,1)} %hidden_in.1, f32[4608]{0:T(1024)} %pre_gain_in.1, ...), custom_call_target="tpu_custom_call" | custom-call | tf_op jit(solution)/shard_map/pallas_call | solution.py:625
  46.8 1.5 %copy.17 = bf16[32,1152]{1,0:T(8,128)(2,1)} copy(bf16[32,1152]{1,0:T(8,128)(2,1)} %get-tuple-element.4) | data formatting | bytes 147456
  48.3 1.5 %copy.18 = bf16[32,2,512]{2,1,0:T(2,128)(2,1)} copy(bf16[32,2,512]{2,1,0:T(2,128)(2,1)} %get-tuple-element.5) | data formatting | bytes 131072

commit v2 on v1

--- a/solution.py
+++ b/solution.py
@@ -188,67 +188,84 @@
 TOKENS = 128
 
 
-def attend_groups(groups, heads, kv_heads, hd, score_scale):
+def stacked(x, count):
+    return jnp.concatenate([x] * count, axis=0)
+
+
+def slot_unit(per):
+    return lax.broadcasted_iota(jnp.int32, (SLOTS, TOKENS), 0) // per
+
+
+def group_scores(sizes, qwide, keys, values, pairs, per, live):
+    heads, kv_heads, hd, score_scale = sizes
     tiles = kv_heads * hd // 256
     tile_heads = heads // tiles
     rows = tile_heads * SLOTS
-    slot = lax.broadcasted_iota(jnp.int32, (SLOTS, TOKENS), 0)
-
-    def stacked(x):
-        return jnp.concatenate([x] * tile_heads, axis=0)
-
-    scores = []
-    for qwide, keys, values, pairs, per, live in groups:
-        unit = stacked(slot // per)
-        chosen = [None] * tiles
+    unit = stacked(slot_unit(per), tile_heads)
+    across = lax.broadcasted_iota(jnp.int32, (TOKENS, tiles * rows), 1) % SLOTS // per
+    held, streamed = [None] * tiles, None
+    for pair in range(pairs):
+        raws = []
+        for t in range(tiles):
+            q = qwide[t * rows : (t + 1) * rows, t * 256 : (t + 1) * 256]
+            two = (keys(pair, t), q) if pair % 2 == 0 else (q, keys(pair, t))
+            raws.append(
+                lax.dot_general(
+                    *two, (((1,), (1,)), ((), ())), preferred_element_type=jnp.float32
+                )
+            )
+        if pair % 2 == 0:
+            raw = jnp.concatenate(raws, axis=1)
+            for u in range(2):
+                part = raw[u * TOKENS : (u + 1) * TOKENS]
+                streamed = part if streamed is None else jnp.where(
+                    across == 2 * pair + u, part, streamed
+                )
+        else:
+            for t in range(tiles):
+                for u in range(2):
+                    part = raws[t][:, u * TOKENS : (u + 1) * TOKENS]
+                    held[t] = part if held[t] is None else jnp.where(
+                        unit == 2 * pair + u, part, held[t]
+                    )
+    turned = streamed.T
+    from_streamed = unit // 2 % 2 == 0
+    return [
+        jnp.where(from_streamed, turned[t * rows : (t + 1) * rows], held[t]) for t in range(tiles)
+    ]
+
+
+def group_mixes(sizes, chosen, qwide, keys, values, pairs, per, live):
+    heads, kv_heads, hd, score_scale = sizes
+    tiles = kv_heads * hd // 256
+    tile_heads = heads // tiles
+    wide_live = stacked(live, tile_heads)
+    mixes, totals = [], []
+    for t in range(tiles):
+        weight = jnp.exp(cap_limit * jnp.tanh(chosen[t] * (score_scale / cap_limit)))
+        weight = jnp.where(wide_live > 0, weight, 0.0)
+        total = jnp.sum(weight, axis=1, keepdims=True)
+        narrow = weight.astype(jnp.bfloat16)
+        acc = None
         for pair in range(pairs):
-            for t in range(tiles):
-                raw = lax.dot_general(
-                    qwide[t * rows : (t + 1) * rows, t * 256 : (t + 1) * 256],
-                    keys(pair, t),
-                    (((1,), (1,)), ((), ())),
-                    preferred_element_type=jnp.float32,
-                )
-                for u in range(2):
-                    part = raw[:, u * TOKENS : (u + 1) * TOKENS]
-                    if chosen[t] is None:
-                        chosen[t] = part
-                    else:
-                        chosen[t] = jnp.where(unit == 2 * pair + u, part, chosen[t])
-        scores.append(chosen)
-    results = []
-    for chosen, (qwide, keys, values, pairs, per, live) in zip(scores, groups):
-        wide_live = stacked(live)
-        mixes, totals = [], []
-        for t in range(tiles):
-            weight = jnp.exp(cap_limit * jnp.tanh(chosen[t] * (score_scale / cap_limit)))
-            weight = jnp.where(wide_live > 0, weight, 0.0)
-            total = jnp.sum(weight, axis=1, keepdims=True)
-            narrow = weight.astype(jnp.bfloat16)
-            acc = None
-            for pair in range(pairs):
-                pieces = []
-                for u in range(2):
-                    keep = (slot // per == 2 * pair + u).astype(jnp.float32).astype(jnp.bfloat16)
-                    pieces.append(narrow * stacked(keep))
-                term = jnp.dot(
-                    jnp.concatenate(pieces, axis=1),
-                    values(pair, t),
-                    preferred_element_type=jnp.float32,
-                )
-                acc = term if acc is None else acc + term
-            group = heads // kv_heads
-            for i in range(tile_heads):
-                span = slice(i * SLOTS, (i + 1) * SLOTS)
-                kv = i // group
-                mixes.append(acc[span, kv * hd : (kv + 1) * hd])
-                totals.append(total[span])
-        lane = lax.broadcasted_iota(jnp.int32, (SLOTS, hd), 1)
-        packed_total = jnp.zeros((SLOTS, hd), jnp.float32)
-        for h in range(heads):
-            packed_total = jnp.where(lane == h, totals[h], packed_total)
-        results.append(mixes + [packed_total])
-    return results
+            pieces = []
+            for u in range(2):
+                keep = (slot_unit(per) == 2 * pair + u).astype(jnp.float32).astype(jnp.bfloat16)
+                pieces.append(narrow * stacked(keep, tile_heads))
+            term = jnp.dot(
+                jnp.concatenate(pieces, axis=1), values(pair, t), preferred_element_type=jnp.float32
+            )
+            acc = term if acc is None else acc + term
+        for i in range(tile_heads):
+            span = slice(i * SLOTS, (i + 1) * SLOTS)
+            kv = i // (heads // kv_heads)
+            mixes.append(acc[span, kv * hd : (kv + 1) * hd])
+            totals.append(total[span])
+    lane = lax.broadcasted_iota(jnp.int32, (SLOTS, hd), 1)
+    packed_total = jnp.zeros((SLOTS, hd), jnp.float32)
+    for h in range(heads):
+        packed_total = jnp.where(lane == h, totals[h], packed_total)
+    return mixes + [packed_total]
 
 
 def layer_kernel(
@@ -310,28 +327,34 @@
     seq_peers = partners(me)
     tensor_peers = partners(mine)
 
-    def w_copy(k):
+    w_rows = w_out.shape[0] // 2
+
+    def w_copy(k, i):
         column = tensor_peers[k] if k < 3 else mine
         start = pl.multiple_of(column * cols, 128)
-        return pltpu.make_async_copy(w_out.at[:, pl.ds(start, cols)], w_buf.at[k], w_sem.at[k])
-
-    smalls[0].start()
-    smalls[1].start()
+        span = pl.ds(i * w_rows, w_rows)
+        return pltpu.make_async_copy(
+            w_out.at[span, pl.ds(start, cols)], w_buf.at[k, span], w_sem.at[2 * k + i]
+        )
+
+    for copy in smalls:
+        copy.start()
+
+    def start_all(count, start_one):
+        def one(i, carry):
+            start_one(i)
+            return carry
+
+        lax.fori_loop(0, count, one, 0)
+
     for n in range(2):
-        for c in range(steps):
-            q_copy(n, c).start()
-        if n == 0:
-            for copy in smalls[2:]:
-                copy.start()
-    for b in range(pages // SLOTS):
-        pool_copy(b).start()
-    for b in range(n_tasks // SLOTS):
-        prompt_copy(b).start()
-    for c in range(steps):
-        kv_copy(w_key, k_buf, k_sem, c).start()
-        kv_copy(w_value, v_buf, v_sem, c).start()
+        start_all(steps, lambda c, n=n: q_copy(n, c).start())
+    start_all(pages // SLOTS, lambda b: pool_copy(b).start())
+    start_all(n_tasks // SLOTS, lambda b: prompt_copy(b).start())
+    start_all(steps, lambda c: kv_copy(w_key, k_buf, k_sem, c).start())
+    start_all(steps, lambda c: kv_copy(w_value, v_buf, v_sem, c).start())
     for k in range(4):
-        w_copy(k).start()
+        start_all(2, lambda i, k=k: w_copy(k, i).start())
 
     barrier = pltpu.get_barrier_semaphore()
     for peer in seq_peers:
@@ -430,74 +453,70 @@
 
     token = lax.broadcasted_iota(jnp.int32, (SLOTS, TOKENS), 1)
 
-    def pool_step(step, carry):
-        groups = []
-        starts = []
-        for s in range(2):
-            g = step * 2 + s
-            pool_copy(g).wait()
-            start = pl.multiple_of(g * SLOTS, SLOTS)
-            widen(s, lambda lanes, start=start: page_query[pl.ds(start, SLOTS), lanes])
-
-            def load(which, start=start):
-                def one(pair, t):
-                    return pool_buf[
-                        pl.ds(start + 2 * pair, 2), which, :, t * 256 : (t + 1) * 256
-                    ].reshape(2 * block_len, 256)
-
-                return one
-
-            live = jnp.where(
-                token.astype(jnp.float32) < valid[pl.ds(start, SLOTS), :], 1.0, 0.0
-            )
-            groups.append((qwide.at[s], load(0), load(1), SLOTS // 2, 1, live))
-            starts.append(start)
-        for start, result in zip(
-            starts, attend_groups(groups, heads, kv_heads, hd, score_scale)
-        ):
-            for i, piece in enumerate(result):
-                page_mix[pl.ds(start, SLOTS), i * hd : (i + 1) * hd] = piece
-        return carry
-
-    lax.fori_loop(0, pages // (2 * SLOTS), pool_step, 0)
-    high = page_mix[...].astype(jnp.bfloat16)
-    both[:pages, :] = high
-    both[pages:, :] = (page_mix[...] - high.astype(jnp.float32)).astype(jnp.bfloat16)
-    req_mix[...] = jnp.dot(onehot_t[...], both[...], preferred_element_type=jnp.float32)
-
-    for b in range(n_tasks // SLOTS):
-        prompt_copy(b).wait()
+    sizes = (heads, kv_heads, hd, score_scale)
     per = TOKENS // prompt_len
     slot_of = lax.broadcasted_iota(jnp.int32, (SLOTS, TOKENS), 0)
     fits = token // prompt_len == slot_of % per
+    pool_groups = pages // SLOTS
+    halves = rows // SLOTS
+    takers = seq_peers + [me]
+
+    def pool_group(g):
+        start = g * SLOTS
+        widen(g % 4, lambda lanes: page_query[start : start + SLOTS, lanes])
+
+        def load(which):
+            def one(pair, t):
+                first = start + 2 * pair
+                return pool_buf[first : first + 2, which, :, t * 256 : (t + 1) * 256].reshape(
+                    2 * block_len, 256
+                )
+
+            return one
+
+        live = jnp.where(token.astype(jnp.float32) < valid[start : start + SLOTS, :], 1.0, 0.0)
+        return (qwide.at[g % 4], load(0), load(1), SLOTS // 2, 1, live)
+
+    def prompt_group(k, s):
+        peer = takers[k]
+        first = peer * rows + s * SLOTS
+        slot = (k % 2) * 2 + s
+        widen(slot, lambda lanes: queries[peer, s * SLOTS : (s + 1) * SLOTS, lanes])
+        places = [
+            jnp.clip(tasks[first + i] - me * n_tasks, 0, n_tasks - 1) for i in range(SLOTS)
+        ]
+
+        def load(which):
+            def one(pair, t):
+                return jnp.concatenate(
+                    [
+                        prompt_buf[place, which, :, t * 256 : (t + 1) * 256]
+                        for place in places[pair * 2 * per : (pair + 1) * 2 * per]
+                    ],
+                    axis=0,
+                )
+
+            return one
+
+        start = pl.multiple_of(first, SLOTS)
+        live = jnp.where(fits, owned[pl.ds(start, SLOTS), :], 0.0)
+        return (qwide.at[slot], load(0), load(1), SLOTS // (2 * per), per, live)
+
+    def scores_of(made):
+        return [(group, group_scores(sizes, *group)) for group in made]
+
+    def finish_pool(g, scored):
+        (group, chosen), = scored
+        for i, piece in enumerate(group_mixes(sizes, chosen, *group)):
+            page_mix[g * SLOTS : (g + 1) * SLOTS, i * hd : (i + 1) * hd] = piece
+
     mix_copies = []
-    for k, peer in enumerate(seq_peers + [me]):
-        groups = []
-        for s in range(rows // SLOTS):
-            first = peer * rows + s * SLOTS
-            widen(s, lambda lanes, s=s: queries[peer, s * SLOTS : (s + 1) * SLOTS, lanes])
-            places = [
-                jnp.clip(tasks[first + i] - me * n_tasks, 0, n_tasks - 1) for i in range(SLOTS)
-            ]
-
-            def load(which, places=places):
-                def one(pair, t):
-                    return jnp.concatenate(
-                        [
-                            prompt_buf[place, which, :, t * 256 : (t + 1) * 256]
-                            for place in places[pair * 2 * per : (pair + 1) * 2 * per]
-                        ],
-                        axis=0,
-                    )
-
-                return one
-
-            start = pl.multiple_of(first, SLOTS)
-            live = jnp.where(fits, owned[pl.ds(start, SLOTS), :], 0.0)
-            groups.append((qwide.at[s], load(0), load(1), SLOTS // (2 * per), per, live))
-        for s, result in enumerate(attend_groups(groups, heads, kv_heads, hd, score_scale)):
+
+    def finish_prompt(k, scored):
+        peer = takers[k]
+        for s, (group, chosen) in enumerate(scored):
             start = pl.multiple_of(peer * rows + s * SLOTS, SLOTS)
-            for i, piece in enumerate(result):
+            for i, piece in enumerate(group_mixes(sizes, chosen, *group)):
                 lanes = slice(i * hd, (i + 1) * hd)
                 sums = req_mix[pl.ds(start, SLOTS), lanes] + piece
                 if k < 3:
@@ -513,8 +532,28 @@
             copy.start()
             mix_copies.append(copy)
 
-    kv_new = []
-    for src, dst, sem in ((w_key, k_buf, k_sem), (w_value, v_buf, v_sem)):
+    scored = None
+    for g in range(pool_groups):
+        pool_copy(g).wait()
+        later = scores_of([pool_group(g)])
+        if g:
+            finish_pool(g - 1, scored)
+        scored = later
+    for b in range(n_tasks // SLOTS):
+        prompt_copy(b).wait()
+    later = scores_of([prompt_group(0, s) for s in range(halves)])
+    finish_pool(pool_groups - 1, scored)
+    high = page_mix[...].astype(jnp.bfloat16)
+    both[:pages, :] = high
+    both[pages:, :] = (page_mix[...] - high.astype(jnp.float32)).astype(jnp.bfloat16)
+    req_mix[...] = jnp.dot(onehot_t[...], both[...], preferred_element_type=jnp.float32)
+    for k in range(1, len(takers)):
+        scored = later
+        later = scores_of([prompt_group(k, s) for s in range(halves)])
+        finish_prompt(k - 1, scored)
+    finish_prompt(len(takers) - 1, later)
+
+    def kv_product(src, dst, sem):
         acc = None
         for c in range(steps):
             kv_copy(src, dst, sem, c).wait()
@@ -524,14 +563,12 @@
                 preferred_element_type=jnp.float32,
             )
             acc = term if acc is None else acc + term
-        kv_new.append(acc)
+        return acc
+
+    key_new = kv_product(w_key, k_buf, k_sem)
     for g in range(kv_heads):
         lanes = slice(g * hd, (g + 1) * hd)
-        fresh[0, :, lanes] = rope_lanes(kv_new[0][:, lanes], cos_all, sin_all).astype(jnp.bfloat16)
-    fresh[1] = kv_new[1].astype(jnp.bfloat16)
-    for i in range(2):
-        fresh_rows[:, i, :] = fresh[i].astype(jnp.float32)
-    fresh_out[...] = fresh_rows[...].astype(jnp.bfloat16)
+        fresh[0, :, lanes] = rope_lanes(key_new[:, lanes], cos_all, sin_all).astype(jnp.bfloat16)
     self_weights = []
     for h in range(heads):
         g = h // group
@@ -539,6 +576,10 @@
         k = fresh[0, :, g * hd : (g + 1) * hd].astype(jnp.float32)
         raw = jnp.sum(q * k, axis=1, keepdims=True)
         self_weights.append(jnp.exp(cap_limit * jnp.tanh(raw * (score_scale / cap_limit))))
+    fresh[1] = kv_product(w_value, v_buf, v_sem).astype(jnp.bfloat16)
+    for i in range(2):
+        fresh_rows[:, i, :] = fresh[i].astype(jnp.float32)
+    fresh_out[...] = fresh_rows[...].astype(jnp.bfloat16)
     for copy in mix_copies:
         copy.wait()
     own = pl.ds(pl.multiple_of(me * rows, SLOTS), rows)
@@ -558,7 +599,8 @@
 
     parts = []
     for k in range(4):
-        w_copy(k).wait()
+        for i in range(2):
+            w_copy(k, i).wait()
         projected = jnp.dot(attended[...], w_buf[k], preferred_element_type=jnp.float32)
         if k < 3:
             sent[k] = projected.astype(jnp.bfloat16)
@@ -602,6 +644,17 @@
 STEPS = 3
 
 
+def place_kernel(layer_in, fresh_in, layer_out, fresh_out, sems):
+    copies = [
+        pltpu.make_async_copy(layer_in, layer_out, sems.at[0]),
+        pltpu.make_async_copy(fresh_in, fresh_out, sems.at[1]),
+    ]
+    for copy in copies:
+        copy.start()
+    for copy in copies:
+        copy.wait()
+
+
 def body(
     seq, tensor, hidden, pre_gain, w_query, w_key, w_value, w_out, post_gain,
     cache_pool, prompt_cache, task_ids, cache_lengths, block_table,
@@ -622,11 +675,11 @@
     dma = pltpu.SemaphoreType.DMA
     bf16, f32, i32 = jnp.bfloat16, jnp.float32, jnp.int32
     packed_width = q_width + HD
-    return pl.pallas_call(
+    layer_out, fresh = pl.pallas_call(
         functools.partial(layer_kernel, seq, tensor, score_scale, HD, STEPS),
         out_shape=(
-            jax.ShapeDtypeStruct((rows, cols), bf16),
-            jax.ShapeDtypeStruct((rows, 2, kv_width), bf16),
+            pltpu.VMEM((rows, cols), bf16),
+            pltpu.VMEM((rows, 2, kv_width), bf16),
         ),
         in_specs=[hbm] * 14,
         out_specs=(vmem, vmem),
@@ -652,7 +705,7 @@
             pltpu.VMEM((pages, TOKENS), f32),
             pltpu.VMEM((requests, TOKENS), f32),
             pltpu.VMEM((pages, q_width), bf16),
-            pltpu.VMEM((2, heads * SLOTS, kv_width), bf16),
+            pltpu.VMEM((4, heads * SLOTS, kv_width), bf16),
             pltpu.VMEM((pages, packed_width), f32),
             pltpu.VMEM((2 * pages, packed_width), bf16),
             pltpu.VMEM((requests, packed_width), f32),
@@ -669,7 +722,7 @@
             dma((2 * STEPS,)),
             dma((STEPS,)),
             dma((STEPS,)),
-            dma((tensor,)),
+            dma((2 * tensor,)),
             dma((pages // SLOTS,)),
             dma((n_tasks // SLOTS,)),
             dma((6,)),
@@ -689,6 +742,17 @@
         hidden, pre_gain, frequency, post_gain,
         w_query, w_key, w_value, w_out, cache_pool, prompt_cache,
     )
+    return pl.pallas_call(
+        place_kernel,
+        out_shape=(
+            jax.ShapeDtypeStruct((rows, cols), bf16),
+            jax.ShapeDtypeStruct((rows, 2, kv_width), bf16),
+        ),
+        in_specs=[vmem, vmem],
+        out_specs=(hbm, hbm),
+        scratch_shapes=[dma((2,))],
+        compiler_params=pltpu.CompilerParams(vmem_limit_bytes=1024 * 1024),
+    )(layer_out, fresh)
 
 
 def fits(seq, tensor, arrays):

time: 50 us -> 34.5 us (0.69)
  Pallas kernels: 46.2 us -> 33.7 us
  local copies, waits for them, and re-layouts: 3.04 us -> 0 us
    pallas_call x1, Pallas kernels: 46.2 us -> 33 us  [body(): pl.pallas_call(functools.partial(layer_kernel, seq, tensor, score_scale,...]
    unnamed x2 -> x0, local copies, waits for them, and re-layouts: 3.04 us -> none
    pallas_call x0 -> x1, Pallas kernels: none -> 0.67 us  [body(): pl.pallas_call(place_kernel, out_shape=(jax.ShapeDtypeStruct((rows, cols)...]
where the time goes in v2:
time: 34.5 us; the launch traced here: 34.3 us
  Pallas kernels  33.7 us (98%)
  between operations  0.64 us (2%)
    pallas_call x1, Pallas kernels, body(): pl.pallas_call(functools.partial(layer_kernel, seq, tensor, score_scale,...  33 us

profile of v2, /device:TPU:0, one launch (start us, length us, event | category | flops | bytes accessed | tf_op | source)
XLA Modules:
  0.0 34.3 jit_solution(5229451011797303637)
XLA Ops:
  0.6 33.0 %shard_map.140 = (bf16[32,1152]{1,0:T(8,128)(2,1)S(1)}, bf16[32,2,512]{2,1,0:T(2,128)(2,1)S(1)}) custom-call(s32[1,128]{1,0:T(1,128)} %bitcast.5, s32[128]{0:T(128)} %tasks_in.1, s32[1,128]{1,0:T(1,128)} %bitcast.4, s32[32,128]{1,0:T(8,128)} %bitcast.3, bf16[32,4608]{1,0:T(8,128)(2,1)} %hidden_in.1, f32[4608]{0:T(1024)} %pre_gain_in.1, ...), custom_call_target="tpu_custom_call" | custom-call | tf_op jit(solution)/shard_map/pallas_call | solution.py:678
  33.6 0.7 %shard_map.141 = (bf16[32,1152]{1,0:T(8,128)(2,1)}, bf16[32,2,512]{2,1,0:T(2,128)(2,1)}) custom-call(bf16[32,1152]{1,0:T(8,128)(2,1)S(1)} %get-tuple-element.4.layer_in, bf16[32,2,512]{2,1,0:T(2,128)(2,1)S(1)} %get-tuple-element.5.fresh_in), custom_call_target="tpu_custom_call" | custom-call | tf_op jit(solution)/shard_map/pallas_call | solution.py:745

commit v3 on v2

--- a/solution.py
+++ b/solution.py
@@ -196,71 +196,64 @@
     return lax.broadcasted_iota(jnp.int32, (SLOTS, TOKENS), 0) // per
 
 
-def group_scores(sizes, qwide, keys, values, pairs, per, live):
+def tile_scores(sizes, t, qwide, keys, values, pairs, per, live):
     heads, kv_heads, hd, score_scale = sizes
-    tiles = kv_heads * hd // 256
-    tile_heads = heads // tiles
+    tile_heads = heads * 256 // (kv_heads * hd)
     rows = tile_heads * SLOTS
     unit = stacked(slot_unit(per), tile_heads)
-    across = lax.broadcasted_iota(jnp.int32, (TOKENS, tiles * rows), 1) % SLOTS // per
-    held, streamed = [None] * tiles, None
+    across = lax.broadcasted_iota(jnp.int32, (TOKENS, rows), 1) % SLOTS // per
+    q = qwide[t * rows : (t + 1) * rows, t * 256 : (t + 1) * 256]
+    held, streamed = None, None
     for pair in range(pairs):
-        raws = []
-        for t in range(tiles):
-            q = qwide[t * rows : (t + 1) * rows, t * 256 : (t + 1) * 256]
-            two = (keys(pair, t), q) if pair % 2 == 0 else (q, keys(pair, t))
-            raws.append(
-                lax.dot_general(
-                    *two, (((1,), (1,)), ((), ())), preferred_element_type=jnp.float32
-                )
-            )
-        if pair % 2 == 0:
-            raw = jnp.concatenate(raws, axis=1)
-            for u in range(2):
+        two = (keys(pair, t), q) if pair % 2 == 0 else (q, keys(pair, t))
+        raw = lax.dot_general(
+            *two, (((1,), (1,)), ((), ())), preferred_element_type=jnp.float32
+        )
+        for u in range(2):
+            if pair % 2 == 0:
                 part = raw[u * TOKENS : (u + 1) * TOKENS]
                 streamed = part if streamed is None else jnp.where(
                     across == 2 * pair + u, part, streamed
                 )
-        else:
-            for t in range(tiles):
-                for u in range(2):
-                    part = raws[t][:, u * TOKENS : (u + 1) * TOKENS]
-                    held[t] = part if held[t] is None else jnp.where(
-                        unit == 2 * pair + u, part, held[t]
-                    )
-    turned = streamed.T
-    from_streamed = unit // 2 % 2 == 0
-    return [
-        jnp.where(from_streamed, turned[t * rows : (t + 1) * rows], held[t]) for t in range(tiles)
-    ]
-
-
-def group_mixes(sizes, chosen, qwide, keys, values, pairs, per, live):
+            else:
+                part = raw[:, u * TOKENS : (u + 1) * TOKENS]
+                held = part if held is None else jnp.where(unit == 2 * pair + u, part, held)
+    return jnp.where(unit // 2 % 2 == 0, streamed.T, held)
+
+
+def tile_mixes(sizes, chosen, t, qwide, keys, values, pairs, per, live):
     heads, kv_heads, hd, score_scale = sizes
-    tiles = kv_heads * hd // 256
-    tile_heads = heads // tiles
-    wide_live = stacked(live, tile_heads)
+    tile_heads = heads * 256 // (kv_heads * hd)
+    weight = jnp.exp(cap_limit * jnp.tanh(chosen * (score_scale / cap_limit)))
+    weight = jnp.where(stacked(live, tile_heads) > 0, weight, 0.0)
+    total = jnp.sum(weight, axis=1, keepdims=True)
+    narrow = weight.astype(jnp.bfloat16)
+    acc = None
+    for pair in range(pairs):
+        pieces = []
+        for u in range(2):
+            keep = (slot_unit(per) == 2 * pair + u).astype(jnp.float32).astype(jnp.bfloat16)
+            pieces.append(narrow * stacked(keep, tile_heads))
+        term = jnp.dot(
+            jnp.concatenate(pieces, axis=1), values(pair, t), preferred_element_type=jnp.float32
+        )
+        acc = term if acc is None else acc + term
     mixes, totals = [], []
-    for t in range(tiles):
-        weight = jnp.exp(cap_limit * jnp.tanh(chosen[t] * (score_scale / cap_limit)))
-        weight = jnp.where(wide_live > 0, weight, 0.0)
-        total = jnp.sum(weight, axis=1, keepdims=True)
-        narrow = weight.astype(jnp.bfloat16)
-        acc = None
-        for pair in range(pairs):
-            pieces = []
-            for u in range(2):
-                keep = (slot_unit(per) == 2 * pair + u).astype(jnp.float32).astype(jnp.bfloat16)
-                pieces.append(narrow * stacked(keep, tile_heads))
-            term = jnp.dot(
-                jnp.concatenate(pieces, axis=1), values(pair, t), preferred_element_type=jnp.float32
-            )
-            acc = term if acc is None else acc + term
-        for i in range(tile_heads):
-            span = slice(i * SLOTS, (i + 1) * SLOTS)
-            kv = i // (heads // kv_heads)
-            mixes.append(acc[span, kv * hd : (kv + 1) * hd])
-            totals.append(total[span])
+    for i in range(tile_heads):
+        span = slice(i * SLOTS, (i + 1) * SLOTS)
+        kv = i // (heads // kv_heads)
+        mixes.append(acc[span, kv * hd : (kv + 1) * hd])
+        totals.append(total[span])
+    return mixes, totals
+
+
+def group_mixes(sizes, scores, group):
+    heads, hd = sizes[0], sizes[2]
+    mixes, totals = [], []
+    for t, chosen in enumerate(scores):
+        more = tile_mixes(sizes, chosen, t, *group)
+        mixes += more[0]
+        totals += more[1]
     lane = lax.broadcasted_iota(jnp.int32, (SLOTS, hd), 1)
     packed_total = jnp.zeros((SLOTS, hd), jnp.float32)
     for h in range(heads):
@@ -276,7 +269,7 @@
     lengths, tasks, tasks_row, table, hidden, pre_gain, frequency, post_gain,
     normed, queries, q_buf, k_buf, v_buf, w_buf, pool_buf, prompt_buf,
     onehot, onehot_t, valid, owned, page_query, qwide, page_mix, both, req_mix, packed, landed,
-    fresh, fresh_rows, attended, sent, arrived, square, squares,
+    fresh, fresh_rows, attended, sent, arrived, held, whole_sum, square, squares,
     small_sem, q_sem, k_sem, v_sem, w_sem, pool_sem, prompt_sem,
     query_send, query_recv, mix_send, mix_recv, part_send, part_recv, square_send, square_recv,
 ):
@@ -294,6 +287,7 @@
     max_blocks = table.shape[0]
     half = q_width // 2
     chunk = depth // steps
+    cut = cols // 256 * 128
 
     smalls = []
     for i, (src, dst) in enumerate((
@@ -325,7 +319,7 @@
         return [3 - i, lax.rem(i + 2, 4), i + 1 - 2 * lax.rem(i, 2)]
 
     seq_peers = partners(me)
-    tensor_peers = partners(mine)
+    tensor_peers = [lax.rem(mine + 2, 4), 3 - mine, mine + 1 - 2 * lax.rem(mine, 2)]
 
     w_rows = w_out.shape[0] // 2
 
@@ -437,23 +431,10 @@
         jnp.sum(jnp.where(line == across, is_owned, 0.0), axis=1, keepdims=True), owned.shape
     )
 
-    for copy in query_copies:
-        copy.wait()
-    all_queries = queries[...].reshape(requests, q_width)
-    page_query[...] = jnp.dot(
-        onehot[...], all_queries, preferred_element_type=jnp.float32
-    ).astype(jnp.bfloat16)
-
-    def widen(slot, source):
-        for h in range(heads):
-            kv = h // group
-            qwide[slot, h * SLOTS : (h + 1) * SLOTS, kv * hd : (kv + 1) * hd] = source(
-                slice(h * hd, (h + 1) * hd)
-            )
-
+    sizes = (heads, kv_heads, hd, score_scale)
+    tiles = kv_width // 256
+    tile_heads = heads // tiles
     token = lax.broadcasted_iota(jnp.int32, (SLOTS, TOKENS), 1)
-
-    sizes = (heads, kv_heads, hd, score_scale)
     per = TOKENS // prompt_len
     slot_of = lax.broadcasted_iota(jnp.int32, (SLOTS, TOKENS), 0)
     fits = token // prompt_len == slot_of % per
@@ -461,9 +442,15 @@
     halves = rows // SLOTS
     takers = seq_peers + [me]
 
+    def widen(slot, t, source):
+        for h in range(t * tile_heads, (t + 1) * tile_heads):
+            kv = h // group
+            qwide[slot, h * SLOTS : (h + 1) * SLOTS, kv * hd : (kv + 1) * hd] = source(
+                slice(h * hd, (h + 1) * hd)
+            )
+
     def pool_group(g):
         start = g * SLOTS
-        widen(g % 4, lambda lanes: page_query[start : start + SLOTS, lanes])
 
         def load(which):
             def one(pair, t):
@@ -477,11 +464,13 @@
         live = jnp.where(token.astype(jnp.float32) < valid[start : start + SLOTS, :], 1.0, 0.0)
         return (qwide.at[g % 4], load(0), load(1), SLOTS // 2, 1, live)
 
-    def prompt_group(k, s):
-        peer = takers[k]
+    def pool_scores(made, g, t):
+        widen(g % 4, t, lambda lanes: page_query[g * SLOTS : (g + 1) * SLOTS, lanes])
+        return tile_scores(sizes, t, *made)
+
+    def prompt_group(n):
+        peer, s = takers[n // halves], n % halves
         first = peer * rows + s * SLOTS
-        slot = (k % 2) * 2 + s
-        widen(slot, lambda lanes: queries[peer, s * SLOTS : (s + 1) * SLOTS, lanes])
         places = [
             jnp.clip(tasks[first + i] - me * n_tasks, 0, n_tasks - 1) for i in range(SLOTS)
         ]
@@ -500,58 +489,80 @@
 
         start = pl.multiple_of(first, SLOTS)
         live = jnp.where(fits, owned[pl.ds(start, SLOTS), :], 0.0)
-        return (qwide.at[slot], load(0), load(1), SLOTS // (2 * per), per, live)
-
-    def scores_of(made):
-        return [(group, group_scores(sizes, *group)) for group in made]
-
-    def finish_pool(g, scored):
-        (group, chosen), = scored
-        for i, piece in enumerate(group_mixes(sizes, chosen, *group)):
+        return (qwide.at[n % 4], load(0), load(1), SLOTS // (2 * per), per, live)
+
+    def prompt_scores(made, n):
+        peer, s = takers[n // halves], n % halves
+        scores = []
+        for t in range(tiles):
+            widen(n % 4, t, lambda lanes: queries[peer, s * SLOTS : (s + 1) * SLOTS, lanes])
+            scores.append(tile_scores(sizes, t, *made))
+        return scores
+
+    def finish_pool(g, made, scores):
+        for i, piece in enumerate(group_mixes(sizes, scores, made)):
             page_mix[g * SLOTS : (g + 1) * SLOTS, i * hd : (i + 1) * hd] = piece
 
     mix_copies = []
 
-    def finish_prompt(k, scored):
+    def finish_prompt(n, made, scores):
+        k, s = n // halves, n % halves
         peer = takers[k]
-        for s, (group, chosen) in enumerate(scored):
-            start = pl.multiple_of(peer * rows + s * SLOTS, SLOTS)
-            for i, piece in enumerate(group_mixes(sizes, chosen, *group)):
-                lanes = slice(i * hd, (i + 1) * hd)
-                sums = req_mix[pl.ds(start, SLOTS), lanes] + piece
-                if k < 3:
-                    packed[k, s * SLOTS : (s + 1) * SLOTS, lanes] = sums.astype(jnp.bfloat16)
-                else:
-                    req_mix[pl.ds(start, SLOTS), lanes] = sums
+        span = slice(s * SLOTS, (s + 1) * SLOTS)
+        start = pl.multiple_of(peer * rows + s * SLOTS, SLOTS)
+        for i, piece in enumerate(group_mixes(sizes, scores, made)):
+            lanes = slice(i * hd, (i + 1) * hd)
+            sums = req_mix[pl.ds(start, SLOTS), lanes] + piece
+            if k < 3:
+                packed[k, span, lanes] = sums.astype(jnp.bfloat16)
+            else:
+                req_mix[pl.ds(start, SLOTS), lanes] = sums
         if k < 3:
             copy = pltpu.make_async_remote_copy(
-                src_ref=packed.at[k], dst_ref=landed.at[k],
-                send_sem=mix_send.at[k], recv_sem=mix_recv.at[k],
+                src_ref=packed.at[k, span], dst_ref=landed.at[k, span],
+                send_sem=mix_send.at[n], recv_sem=mix_recv.at[n],
                 device_id={"seq": peer}, device_id_type=MESH,
             )
             copy.start()
             mix_copies.append(copy)
 
-    scored = None
+    pools = [pool_group(g) for g in range(pool_groups)]
+    early = 2
+    scores = [[] for _ in pools]
+    for t in range(tiles):
+        for copy in query_copies[3 * t : 3 * (t + 1)]:
+            copy.wait()
+        lanes = slice(t * half, (t + 1) * half)
+        page_query[:, lanes] = jnp.dot(
+            onehot[...], queries[:, :, lanes].reshape(requests, half),
+            preferred_element_type=jnp.float32,
+        ).astype(jnp.bfloat16)
+        if t == 0:
+            for g in range(early):
+                pool_copy(g).wait()
+                scores[g].append(pool_scores(pools[g], g, t))
     for g in range(pool_groups):
-        pool_copy(g).wait()
-        later = scores_of([pool_group(g)])
+        if g >= early:
+            pool_copy(g).wait()
+        for t in range(len(scores[g]), tiles):
+            scores[g].append(pool_scores(pools[g], g, t))
         if g:
-            finish_pool(g - 1, scored)
-        scored = later
-    for b in range(n_tasks // SLOTS):
-        prompt_copy(b).wait()
-    later = scores_of([prompt_group(0, s) for s in range(halves)])
-    finish_pool(pool_groups - 1, scored)
+            finish_pool(g - 1, pools[g - 1], scores[g - 1])
+    finish_pool(pool_groups - 1, pools[-1], scores[-1])
     high = page_mix[...].astype(jnp.bfloat16)
     both[:pages, :] = high
     both[pages:, :] = (page_mix[...] - high.astype(jnp.float32)).astype(jnp.bfloat16)
     req_mix[...] = jnp.dot(onehot_t[...], both[...], preferred_element_type=jnp.float32)
-    for k in range(1, len(takers)):
-        scored = later
-        later = scores_of([prompt_group(k, s) for s in range(halves)])
-        finish_prompt(k - 1, scored)
-    finish_prompt(len(takers) - 1, later)
+    for b in range(n_tasks // SLOTS):
+        prompt_copy(b).wait()
+    made = prompt_group(0)
+    ahead = (made, prompt_scores(made, 0))
+    for n in range(1, len(takers) * halves):
+        made = prompt_group(n)
+        later = (made, prompt_scores(made, n))
+        finish_prompt(n - 1, *ahead)
+        ahead = later
+    finish_prompt(len(takers) * halves - 1, *ahead)
 
     def kv_product(src, dst, sem):
         acc = None
@@ -597,24 +608,66 @@
         mix += rounded * fresh[1, :, g * hd : (g + 1) * hd].astype(jnp.float32)
         attended[:, lanes] = (mix / total).astype(jnp.bfloat16)
 
-    parts = []
-    for k in range(4):
-        for i in range(2):
-            w_copy(k, i).wait()
-        projected = jnp.dot(attended[...], w_buf[k], preferred_element_type=jnp.float32)
-        if k < 3:
-            sent[k] = projected.astype(jnp.bfloat16)
-            copy = pltpu.make_async_remote_copy(
-                src_ref=sent.at[k], dst_ref=arrived.at[k],
-                send_sem=part_send.at[k], recv_sem=part_recv.at[k],
-                device_id={"tensor": tensor_peers[k]}, device_id_type=MESH,
-            )
+    is_inner = lax.rem(mine, 3) != 0
+    onward = lax.rem(2 * mine + 1, 5)
+    pieces = (slice(0, cut), slice(cut, cols))
+
+    def project(k, piece):
+        return jnp.dot(attended[...], w_buf[k, :, piece], preferred_element_type=jnp.float32)
+
+    def part(i, k, piece, peer):
+        return pltpu.make_async_remote_copy(
+            src_ref=sent.at[k, :, piece], dst_ref=arrived.at[k, :, piece],
+            send_sem=part_send.at[i], recv_sem=part_recv.at[i],
+            device_id={"tensor": peer}, device_id_type=MESH,
+        )
+
+    handed = [part(i, 0, pieces[i], onward) for i in range(2)]
+    mirrored = [part(2 + i, 1, pieces[i], tensor_peers[1]) for i in range(2)]
+    beside = part(4, 2, slice(0, cols), tensor_peers[2])
+    for i in range(2):
+        w_copy(0, i).wait()
+    for piece, copy in zip(pieces, handed):
+        sent[0, :, piece] = project(0, piece).astype(jnp.bfloat16)
+        copy.start()
+    for i in range(2):
+        w_copy(1, i).wait()
+    for piece, copy in zip(pieces, mirrored):
+        held[:, piece] = project(1, piece)
+
+        @pl.when(jnp.logical_not(is_inner))
+        def _():
+            sent[1, :, piece] = held[:, piece].astype(jnp.bfloat16)
             copy.start()
-            parts.append(copy)
-    whole = projected
-    for k in (2, 0, 1):
-        parts[k].wait()
-        whole += arrived[k].astype(jnp.float32)
+
+    for i in range(2):
+        w_copy(2, i).wait()
+    sent[2] = project(2, slice(0, cols)).astype(jnp.bfloat16)
+    beside.start()
+    for i in range(2):
+        w_copy(3, i).wait()
+    whole_sum[...] = project(3, slice(0, cols))
+    for piece, take, copy in zip(pieces, handed, mirrored):
+
+        @pl.when(is_inner)
+        def _():
+            take.wait_recv()
+            total = held[:, piece] + arrived[0, :, piece].astype(jnp.float32)
+            sent[1, :, piece] = total.astype(jnp.bfloat16)
+            copy.start()
+
+    beside.wait_recv()
+    whole_sum[...] += arrived[2].astype(jnp.float32)
+
+    @pl.when(jnp.logical_not(is_inner))
+    def _():
+        for copy in handed:
+            copy.wait_recv()
+        whole_sum[...] += arrived[0].astype(jnp.float32)
+
+    for copy in mirrored:
+        copy.wait_recv()
+    whole = whole_sum[...] + arrived[1].astype(jnp.float32)
     part_square = jnp.sum(whole * whole, axis=1, keepdims=True)
     row = lax.broadcasted_iota(jnp.int32, (rows, 128), 0)
     diagonal = row == lax.broadcasted_iota(jnp.int32, (rows, 128), 1)
@@ -639,6 +692,8 @@
     column_square = jnp.sum(jnp.where(diagonal, total_square, 0.0), axis=1, keepdims=True)
     factor = lax.rsqrt(column_square / (cols * tensor) + 1e-06)
     out[...] = (residual + scaled * factor).astype(jnp.bfloat16)
+    for copy in handed + mirrored + [beside]:
+        copy.wait_send()
 
 
 STEPS = 3
@@ -716,6 +771,8 @@
             pltpu.VMEM((rows, q_width), bf16),
             pltpu.VMEM((3, rows, cols), bf16),
             pltpu.VMEM((3, rows, cols), bf16),
+            pltpu.VMEM((rows, cols), f32),
+            pltpu.VMEM((rows, cols), f32),
             pltpu.VMEM((1, 128), f32),
             pltpu.VMEM((3, 1, 128), f32),
             dma((8,)),
@@ -727,10 +784,10 @@
             dma((n_tasks // SLOTS,)),
             dma((6,)),
             dma((6,)),
-            dma((3,)),
-            dma((3,)),
-            dma((3,)),
-            dma((3,)),
+            dma((6,)),
+            dma((6,)),
+            dma((5,)),
+            dma((5,)),
             dma((3,)),
             dma((3,)),
         ],
@@ -763,9 +820,8 @@
         and tensor == 4
         and hidden.shape[0] == 2 * SLOTS
         and hidden.shape[1] % (STEPS * 256) == 0
-        and w_query.shape[1] % 256 == 0
-        and w_key.shape[1] % 256 == 0
-        and w_query.shape[1] % w_key.shape[1] == 0
+        and w_query.shape[1] == 8 * HD
+        and w_key.shape[1] == 4 * HD
         and post_gain.shape[0] % 128 == 0
         and pool.shape[0] == 64
         and pool.shape[2] == TOKENS

time: 34.5 us -> 33.6 us (0.974)
  Pallas kernels: 33.7 us -> 32.8 us
    pallas_call x1, Pallas kernels: 33 us -> 32.1 us  [body(): pl.pallas_call(functools.partial(layer_kernel, seq, tensor, score_scale,...]
where the time goes in v3:
time: 33.6 us; the launch traced here: 33.5 us
  Pallas kernels  32.8 us (98%)
  between operations  0.64 us (2%)
    pallas_call x1, Pallas kernels, body(): pl.pallas_call(functools.partial(layer_kernel, seq, tensor, score_scale,...  32.1 us
    pallas_call x1, Pallas kernels, body(): pl.pallas_call(place_kernel, out_shape=(jax.ShapeDtypeStruct((rows, cols)...  0.67 us

profile of v3, /device:TPU:0, one launch (start us, length us, event | category | flops | bytes accessed | tf_op | source)
XLA Modules:
  0.0 33.5 jit_solution(4424385381125483398)
XLA Ops:
  0.6 32.1 %shard_map.140 = (bf16[32,1152]{1,0:T(8,128)(2,1)S(1)}, bf16[32,2,512]{2,1,0:T(2,128)(2,1)S(1)}) custom-call(s32[1,128]{1,0:T(1,128)} %bitcast.5, s32[128]{0:T(128)} %tasks_in.1, s32[1,128]{1,0:T(1,128)} %bitcast.4, s32[32,128]{1,0:T(8,128)} %bitcast.3, bf16[32,4608]{1,0:T(8,128)(2,1)} %hidden_in.1, f32[4608]{0:T(1024)} %pre_gain_in.1, ...), custom_call_target="tpu_custom_call" | custom-call | tf_op jit(solution)/shard_map/pallas_call | solution.py:733
  32.8 0.7 %shard_map.141 = (bf16[32,1152]{1,0:T(8,128)(2,1)}, bf16[32,2,512]{2,1,0:T(2,128)(2,1)}) custom-call(bf16[32,1152]{1,0:T(8,128)(2,1)S(1)} %get-tuple-element.4.layer_in, bf16[32,2,512]{2,1,0:T(2,128)(2,1)S(1)} %get-tuple-element.5.fresh_in), custom_call_target="tpu_custom_call" | custom-call | tf_op jit(solution)/shard_map/pallas_call | solution.py:802

commit v4 on v3

--- a/solution.py
+++ b/solution.py
@@ -577,6 +577,7 @@
         return acc
 
     key_new = kv_product(w_key, k_buf, k_sem)
+    value_new = kv_product(w_value, v_buf, v_sem)
     for g in range(kv_heads):
         lanes = slice(g * hd, (g + 1) * hd)
         fresh[0, :, lanes] = rope_lanes(key_new[:, lanes], cos_all, sin_all).astype(jnp.bfloat16)
@@ -587,7 +588,7 @@
         k = fresh[0, :, g * hd : (g + 1) * hd].astype(jnp.float32)
         raw = jnp.sum(q * k, axis=1, keepdims=True)
         self_weights.append(jnp.exp(cap_limit * jnp.tanh(raw * (score_scale / cap_limit))))
-    fresh[1] = kv_product(w_value, v_buf, v_sem).astype(jnp.bfloat16)
+    fresh[1] = value_new.astype(jnp.bfloat16)
     for i in range(2):
         fresh_rows[:, i, :] = fresh[i].astype(jnp.float32)
     fresh_out[...] = fresh_rows[...].astype(jnp.bfloat16)
@@ -622,48 +623,49 @@
             device_id={"tensor": peer}, device_id_type=MESH,
         )
 
-    handed = [part(i, 0, pieces[i], onward) for i in range(2)]
+    handed = [part(0, 0, pieces[0], onward), part(1, 0, pieces[1], tensor_peers[0])]
     mirrored = [part(2 + i, 1, pieces[i], tensor_peers[1]) for i in range(2)]
     beside = part(4, 2, slice(0, cols), tensor_peers[2])
-    for i in range(2):
-        w_copy(0, i).wait()
-    for piece, copy in zip(pieces, handed):
-        sent[0, :, piece] = project(0, piece).astype(jnp.bfloat16)
+    for k in range(4):
+        for i in range(2):
+            w_copy(k, i).wait()
+
+    def ship(k, piece, product, copy):
+        sent[k, :, piece] = product.astype(jnp.bfloat16)
         copy.start()
-    for i in range(2):
-        w_copy(1, i).wait()
-    for piece, copy in zip(pieces, mirrored):
-        held[:, piece] = project(1, piece)
-
-        @pl.when(jnp.logical_not(is_inner))
-        def _():
-            sent[1, :, piece] = held[:, piece].astype(jnp.bfloat16)
-            copy.start()
-
-    for i in range(2):
-        w_copy(2, i).wait()
-    sent[2] = project(2, slice(0, cols)).astype(jnp.bfloat16)
-    beside.start()
-    for i in range(2):
-        w_copy(3, i).wait()
-    whole_sum[...] = project(3, slice(0, cols))
-    for piece, take, copy in zip(pieces, handed, mirrored):
-
-        @pl.when(is_inner)
-        def _():
-            take.wait_recv()
-            total = held[:, piece] + arrived[0, :, piece].astype(jnp.float32)
-            sent[1, :, piece] = total.astype(jnp.bfloat16)
-            copy.start()
+
+    whole_piece = slice(0, cols)
+    first = project(0, pieces[0])
+    second = project(0, pieces[1])
+    ship(0, pieces[0], first, handed[0])
+    third = project(1, pieces[1])
+    ship(0, pieces[1], second, handed[1])
+    held[...] = project(1, pieces[0])
+    ship(1, pieces[1], third, mirrored[1])
+
+    @pl.when(jnp.logical_not(is_inner))
+    def _():
+        ship(1, pieces[0], held[...], mirrored[0])
+
+    fourth = project(2, whole_piece)
+    whole_sum[...] = project(3, whole_piece)
+    ship(2, whole_piece, fourth, beside)
+    @pl.when(is_inner)
+    def _():
+        handed[0].wait_recv()
+        total = held[...] + arrived[0, :, pieces[0]].astype(jnp.float32)
+        sent[1, :, pieces[0]] = total.astype(jnp.bfloat16)
+        mirrored[0].start()
 
     beside.wait_recv()
     whole_sum[...] += arrived[2].astype(jnp.float32)
+    handed[1].wait_recv()
+    whole_sum[:, pieces[1]] += arrived[0, :, pieces[1]].astype(jnp.float32)
 
     @pl.when(jnp.logical_not(is_inner))
     def _():
-        for copy in handed:
-            copy.wait_recv()
-        whole_sum[...] += arrived[0].astype(jnp.float32)
+        handed[0].wait_recv()
+        whole_sum[:, pieces[0]] += arrived[0, :, pieces[0]].astype(jnp.float32)
 
     for copy in mirrored:
         copy.wait_recv()
@@ -771,7 +773,7 @@
             pltpu.VMEM((rows, q_width), bf16),
             pltpu.VMEM((3, rows, cols), bf16),
             pltpu.VMEM((3, rows, cols), bf16),
-            pltpu.VMEM((rows, cols), f32),
+            pltpu.VMEM((rows, cols // 256 * 128), f32),
             pltpu.VMEM((rows, cols), f32),
             pltpu.VMEM((1, 128), f32),
             pltpu.VMEM((3, 1, 128), f32),

time: 33.6 us -> 33.3 us (level)
  no operation moved by 1% of the time
where the time goes in v4:
time: 33.3 us; the launch traced here: 33.1 us
  Pallas kernels  32.5 us (98%)
  between operations  0.64 us (2%)
    pallas_call x1, Pallas kernels, body(): pl.pallas_call(functools.partial(layer_kernel, seq, tensor, score_scale,...  31.8 us
    pallas_call x1, Pallas kernels, body(): pl.pallas_call(place_kernel, out_shape=(jax.ShapeDtypeStruct((rows, cols)...  0.67 us

profile of v4, /device:TPU:0, one launch (start us, length us, event | category | flops | bytes accessed | tf_op | source)
XLA Modules:
  0.0 33.1 jit_solution(9624682337865138917)
XLA Ops:
  0.6 31.8 %shard_map.140 = (bf16[32,1152]{1,0:T(8,128)(2,1)S(1)}, bf16[32,2,512]{2,1,0:T(2,128)(2,1)S(1)}) custom-call(s32[1,128]{1,0:T(1,128)} %bitcast.5, s32[128]{0:T(128)} %tasks_in.1, s32[1,128]{1,0:T(1,128)} %bitcast.4, s32[32,128]{1,0:T(8,128)} %bitcast.3, bf16[32,4608]{1,0:T(8,128)(2,1)} %hidden_in.1, f32[4608]{0:T(1024)} %pre_gain_in.1, ...), custom_call_target="tpu_custom_call" | custom-call | tf_op jit(solution)/shard_map/pallas_call | solution.py:735
  32.5 0.7 %shard_map.141 = (bf16[32,1152]{1,0:T(8,128)(2,1)}, bf16[32,2,512]{2,1,0:T(2,128)(2,1)}) custom-call(bf16[32,1152]{1,0:T(8,128)(2,1)S(1)} %get-tuple-element.4.layer_in, bf16[32,2,512]{2,1,0:T(2,128)(2,1)S(1)} %get-tuple-element.5.fresh_in), custom_call_target="tpu_custom_call" | custom-call | tf_op jit(solution)/shard_map/pallas_call | solution.py:804

commit v5 on v4

--- a/solution.py
+++ b/solution.py
@@ -698,7 +698,7 @@
         copy.wait_send()
 
 
-STEPS = 3
+STEPS = 6
 
 
 def place_kernel(layer_in, fresh_in, layer_out, fresh_out, sems):

time: 33.3 us -> 33 us (level)
  no operation moved by 1% of the time
where the time goes in v5:
time: 33 us; the launch traced here: 32.9 us
  Pallas kernels  32.2 us (98%)
  between operations  0.64 us (2%)
    pallas_call x1, Pallas kernels, body(): pl.pallas_call(functools.partial(layer_kernel, seq, tensor, score_scale,...  31.6 us
    pallas_call x1, Pallas kernels, body(): pl.pallas_call(place_kernel, out_shape=(jax.ShapeDtypeStruct((rows, cols)...  0.67 us

profile of v5, /device:TPU:0, one launch (start us, length us, event | category | flops | bytes accessed | tf_op | source)
XLA Modules:
  0.0 32.9 jit_solution(18004301282620350935)
XLA Ops:
  0.6 31.6 %shard_map.140 = (bf16[32,1152]{1,0:T(8,128)(2,1)S(1)}, bf16[32,2,512]{2,1,0:T(2,128)(2,1)S(1)}) custom-call(s32[1,128]{1,0:T(1,128)} %bitcast.5, s32[128]{0:T(128)} %tasks_in.1, s32[1,128]{1,0:T(1,128)} %bitcast.4, s32[32,128]{1,0:T(8,128)} %bitcast.3, bf16[32,4608]{1,0:T(8,128)(2,1)} %hidden_in.1, f32[4608]{0:T(1024)} %pre_gain_in.1, ...), custom_call_target="tpu_custom_call" | custom-call | tf_op jit(solution)/shard_map/pallas_call | solution.py:735
  32.2 0.7 %shard_map.141 = (bf16[32,1152]{1,0:T(8,128)(2,1)}, bf16[32,2,512]{2,1,0:T(2,128)(2,1)}) custom-call(bf16[32,1152]{1,0:T(8,128)(2,1)S(1)} %get-tuple-element.4.layer_in, bf16[32,2,512]{2,1,0:T(2,128)(2,1)S(1)} %get-tuple-element.5.fresh_in), custom_call_target="tpu_custom_call" | custom-call | tf_op jit(solution)/shard_map/pallas_call | solution.py:804
